TPU v7x, 32 devices: a whole 2x2x4 slice. The times are simulated.
32 devices in a mesh: dp: 8 (over z, y), cp: 4 (over x, core).
Axes of the slice: x: 2, y: 2, z: 4, core: 2. Of those that a mesh axis runs over, the one named last changes fastest.
Arguments:
- hidden: bfloat16 [128, 1024, 2048], P('dp', 'cp')
- positions: int32 [1024], P('cp')
- w_q: bfloat16 [2048, 2048], replicated
- w_k: bfloat16 [2048, 2048], replicated
- w_v: bfloat16 [2048, 2048], replicated
- w_o: bfloat16 [2048, 2048], replicated
Outputs:
- output 1: bfloat16 [128, 1024, 2048], P('dp', 'cp')
- output 2: float32 [16], replicated
- output 3: bfloat16 [2048, 2048], replicated
- output 4: bfloat16 [2048, 2048], replicated
All inputs are finite; a program needn't handle non-finite values.
Results may differ from a plain program's by a relative error of at most 0.00757875.
Values are sent between devices in bfloat16 or wider.
A program may use at most 1 GiB of HBM per device.

v0:
```python
import jax
import jax.numpy as jnp
from jax import lax
from jax.sharding import PartitionSpec as P

HEAD_DIM = 128
TAU_CLIP = 100.0
ROPE_THETA = 50000.0


def rope_tables(pos_ids):
    half_dim = HEAD_DIM // 2
    inv_freq = jnp.float32(ROPE_THETA) ** (-jnp.arange(half_dim, dtype=jnp.float32) * (2.0 / HEAD_DIM))
    angle = pos_ids.astype(jnp.float32)[:, None] * inv_freq[None, :]
    return jnp.cos(angle)[None, :, None, :], jnp.sin(angle)[None, :, None, :]


def rope_rotate(tensor, cos_t, sin_t):
    half_dim = HEAD_DIM // 2
    lead_half = tensor[..., :half_dim]
    tail_half = tensor[..., half_dim:]
    return jnp.concatenate([lead_half * cos_t - tail_half * sin_t, tail_half * cos_t + lead_half * sin_t], axis=-1)


def project_heads(hidden, pos_ids, w_q, w_k, w_v):
    batch_n, seq_n, _ = hidden.shape
    head_shape = (batch_n, seq_n, w_q.shape[1] // HEAD_DIM, HEAD_DIM)
    cos_t, sin_t = rope_tables(pos_ids)
    q_heads = rope_rotate(jnp.dot(hidden, w_q, preferred_element_type=jnp.float32).reshape(head_shape), cos_t, sin_t).astype(jnp.bfloat16)
    k_heads = rope_rotate(jnp.dot(hidden, w_k, preferred_element_type=jnp.float32).reshape(head_shape), cos_t, sin_t).astype(jnp.bfloat16)
    v_heads = jnp.dot(hidden, w_v, preferred_element_type=jnp.float32).astype(jnp.bfloat16).reshape(head_shape)
    return q_heads, k_heads, v_heads


def empty_state(batch_n, seq_n, n_heads):
    row_shape = (batch_n, n_heads, seq_n)
    return (jnp.full(row_shape, -jnp.inf, jnp.float32), jnp.zeros(row_shape, jnp.float32),
            jnp.zeros((batch_n, seq_n, n_heads, HEAD_DIM), jnp.float32), jnp.full((n_heads,), -jnp.inf, jnp.float32))


def attend_block(q_heads, k_blk, v_blk, state, allowed):
    run_max, run_sum, out_acc, head_max = state
    scores = jnp.einsum("bqhd,bkhd->bhqk", q_heads, k_blk, preferred_element_type=jnp.float32) * (HEAD_DIM ** -0.5)
    if allowed is not None:
        scores = jnp.where(allowed, scores, -jnp.inf)
    head_max = jnp.maximum(head_max, jnp.max(scores, axis=(0, 2, 3)))
    new_max = jnp.maximum(run_max, jnp.max(scores, axis=-1))
    rescale = jnp.exp(run_max - new_max)
    prob_w = jnp.exp(scores - new_max[..., None])
    new_sum = run_sum * rescale + jnp.sum(prob_w, axis=-1)
    part_pv = jnp.einsum("bhqk,bkhd->bqhd", prob_w.astype(jnp.bfloat16), v_blk, preferred_element_type=jnp.float32)
    new_acc = out_acc * jnp.transpose(rescale, (0, 2, 1))[..., None] + part_pv
    return new_max, new_sum, new_acc, head_max


def finish_attn(state, w_o):
    run_max, run_sum, out_acc, head_max = state
    batch_n, seq_n, n_heads, _ = out_acc.shape
    attn_val = (out_acc / jnp.transpose(run_sum, (0, 2, 1))[..., None]).astype(jnp.bfloat16)
    attn_val = attn_val.reshape(batch_n, seq_n, n_heads * HEAD_DIM)
    return jnp.dot(attn_val, w_o, preferred_element_type=jnp.float32).astype(jnp.bfloat16), head_max


def clip_weights(head_max, w_q, w_k):
    factor = jnp.where(head_max > TAU_CLIP, jnp.sqrt(TAU_CLIP / head_max), 1.0)
    col_factor = jnp.repeat(factor, HEAD_DIM)[None, :]
    return (w_q.astype(jnp.float32) * col_factor).astype(jnp.bfloat16), (w_k.astype(jnp.float32) * col_factor).astype(jnp.bfloat16)


def solution(mesh):
    cp_size = mesh.shape["cp"]
    shift_pairs = [(src_rank, (src_rank + 1) % cp_size) for src_rank in range(cp_size)]

    def device_body(hidden, pos_ids, w_q, w_k, w_v, w_o):
        cp_rank = lax.axis_index("cp")
        q_heads, k_heads, v_heads = project_heads(hidden, pos_ids, w_q, w_k, w_v)
        batch_n, seq_n, n_heads, _ = q_heads.shape
        causal = lax.broadcasted_iota(jnp.int32, (seq_n, seq_n), 0) >= lax.broadcasted_iota(jnp.int32, (seq_n, seq_n), 1)
        state = attend_block(q_heads, k_heads, v_heads, empty_state(batch_n, seq_n, n_heads), causal)

        def step(step_idx, carried):
            k_blk, v_blk, attn_state = carried
            k_blk = lax.ppermute(k_blk, "cp", shift_pairs)
            v_blk = lax.ppermute(v_blk, "cp", shift_pairs)

            def use_block(state_in):
                return attend_block(q_heads, k_blk, v_blk, state_in, None)

            def skip_block(state_in):
                return state_in

            attn_state = lax.cond(step_idx <= cp_rank, use_block, skip_block, attn_state)
            return k_blk, v_blk, attn_state

        _, _, state = lax.fori_loop(1, cp_size, step, (k_heads, v_heads, state))
        attn_out, head_max = finish_attn(state, w_o)
        head_max = lax.pmax(head_max, ("dp", "cp"))
        w_q_new, w_k_new = clip_weights(head_max, w_q, w_k)
        return attn_out, head_max, w_q_new, w_k_new

    return jax.shard_map(
        device_body,
        mesh=mesh,
        in_specs=(P("dp", "cp", None), P("cp"), P(None, None), P(None, None), P(None, None), P(None, None)),
        out_specs=(P("dp", "cp", None), P(None), P(None, None), P(None, None)),
        check_vma=False,
    )
```

profile of v0, /device:TPU:0, one launch (start us, length us, event | category | flops | bytes accessed | tf_op | source)
XLA Modules:
  0.0 2169.9 jit_solution(4833661319817586383)
XLA Ops:
  0.6 43.2 %fusion.23 = f32[16,256,2048]{2,1,0:T(8,128)} fusion(bf16[16,256,2048]{2,1,0:T(8,128)(2,1)} %param.10, bf16[2048,2048]{1,0:T(8,128)(2,1)} %param.12), kind=kOutput, calls=%fused_computation.38 | convolution fusion | flops 34359738368 | bytes 58720256 | tf_op jit(solution)/shard_map/dot_general | solution.py:29
  43.8 27.7 %copy.39 = f32[512,8,16,128]{3,2,1,0:T(8,128)} copy(f32[512,8,16,128]{3,1,2,0:T(8,128)} %bitcast.53) | data formatting | bytes 67108864
  71.5 44.7 %fusion.32 = (f32[16,256,16,64]{3,2,1,0:T(8,128)}, f32[16,256,16,64]{3,2,1,0:T(8,128)}) fusion(f32[16,256,16,128]{3,2,1,0:T(8,128)} %bitcast.51), kind=kLoop, calls=%fused_computation.54 | loop fusion | bytes 67108864 | tf_op jit(solution)/shard_map/slice | solution.py:20
  116.2 0.0 slice-done
  116.2 0.0 slice-done.1
  116.2 41.1 %fusion.26 = f32[16,256,2048]{2,1,0:T(8,128)} fusion(bf16[16,256,2048]{2,1,0:T(8,128)(2,1)} %param.10, bf16[2048,2048]{1,0:T(8,128)(2,1)S(1)} %bitcast.59), kind=kOutput, calls=%fused_computation.41 | convolution fusion | flops 34359738368 | bytes 58720256 | tf_op jit(solution)/shard_map/dot_general | solution.py:30
  157.3 27.6 %copy.38 = f32[512,8,16,128]{3,2,1,0:T(8,128)} copy(f32[512,8,16,128]{3,1,2,0:T(8,128)} %bitcast.54) | data formatting | bytes 67108864
  184.8 44.7 %fusion.33 = (f32[16,256,16,64]{3,2,1,0:T(8,128)}, f32[16,256,16,64]{3,2,1,0:T(8,128)}) fusion(f32[16,256,16,128]{3,2,1,0:T(8,128)} %bitcast.52), kind=kLoop, calls=%fused_computation.55 | loop fusion | bytes 67108864 | tf_op jit(solution)/shard_map/slice | solution.py:20
  229.5 0.0 copy-done.1
  229.5 0.5 multiply_cosine_fusion
  230.1 96.4 %subtract_convert_fusion = (bf16[16,256,16,64]{3,1,2,0:T(8,128)(2,1)}, bf16[16,256,16,64]{3,1,2,0:T(8,128)(2,1)}, bf16[16,256,16,64]{3,1,2,0:T(8,128)(2,1)}, bf16[16,256,16,64]{3,1,2,0:T(8,128)(2,1)}) fusion(f32[16,256,16,64]{3,2,1,0:T(8,128)} %get-tuple-element.253, f32[16,256,16,64]{3,2,1,0:T(8,128)} %get-tuple-element.252, ...), kind=kLoop, calls=%fused_computation.26 | loop fusion | flops 67108864 | bytes 100794368 | tf_op jit(solution)/shard_map/convert
  326.4 36.9 %pad_maximum_fusion = (bf16[16,256,16,128]{3,1,2,0:T(8,128)(2,1)}, bf16[16,256,16,128]{3,1,2,0:T(8,128)(2,1)}) fusion(bf16[16,256,16,64]{3,1,2,0:T(8,128)(2,1)} %get-tuple-element.258, bf16[16,256,16,64]{3,1,2,0:T(8,128)(2,1)} %get-tuple-element.259, bf16[16,256,16,64]{3,1,2,0:T(8,128)(2,1)} %get-tuple-element.249, ...), kind=kLoop, calls=%fused_computation.31 | loop fusion | flops 67108864 | bytes 67108864 | tf_op jit(solution)/shard_map/concatenate | solution.py:22
  363.4 33.4 %fusion.13 = (f32[16,16,256]{2,1,0:T(8,128)S(1)}, f32[16,16,256,256]{2,3,1,0:T(8,128)}) fusion(pred[256,256]{0,1:T(8,128)(4,1)S(1)} %iota_compare_fusion, bf16[16,256,16,128]{3,1,2,0:T(8,128)(2,1)} %get-tuple-element.347, bf16[16,256,16,128]{3,1,2,0:T(8,128)(2,1)} %get-tuple-element.340), kind=kOutput, calls=%fused_computation.18 | convolution fusion | flops 4345233408 | bytes 100990976 | tf_op jit(solution)/shard_map/bqhd,bkhd->bhqk/dot_general | solution.py:43
  396.8 25.8 %fusion.12 = (f32[16]{0:T(128)}, f32[16,16,256]{2,1,0:T(8,128)S(1)}) fusion(f32[16,16,256,256]{2,3,1,0:T(8,128)} %get-tuple-element.265, pred[256,256]{0,1:T(8,128)(4,1)S(1)} %iota_compare_fusion, f32[16,16,256]{2,1,0:T(8,128)S(1)} %get-tuple-element.342), kind=kLoop, calls=%fused_computation.17 | loop fusion | flops 83820528 | bytes 67698752 | tf_op jit(solution)/shard_map/reduce_max | solution.py:46
  422.6 0.8 fusion.28
  423.3 41.5 %convert_bitcast_fusion = bf16[16,32,16,8,128]{4,3,2,1,0:T(8,128)(2,1)} fusion(bf16[16,256,2048]{2,1,0:T(8,128)(2,1)} %param.10, bf16[2048,2048]{1,0:T(8,128)(2,1)} %param.14), kind=kOutput, calls=%fused_computation.35 | convolution fusion | flops 34368126976 | bytes 41943040 | tf_op jit(solution)/shard_map/dot_general | solution.py:31
  464.8 43.4 %bitcast_add_fusion.1 = f32[16,256,16,128]{1,3,2,0:T(8,128)} fusion(f32[16,256,16]{1,2,0:T(8,128)S(1)} %get-tuple-element.256, f32[16,16,256,256]{2,3,1,0:T(8,128)} %get-tuple-element.265, f32[16,16,256]{2,1,0:T(8,128)S(1)} %get-tuple-element.342, pred[256,256]{0,1:T(8,128)(4,1)S(1)} %iota_compare_fusion, bf16[16,32,16,8,128]{4,3,2,1,0:T(8,128)(2,1)} %convert_bitcast_fusion), kind=kOutput, calls=%fused_computation.20 | convolution fusion | flops 4370464768 | bytes 118030336 | tf_op jit(solution)/shard_map/bhqk,bkhd->bqhd/dot_general | solution.py:51
  508.3 31.7 %copy.27 = f32[16,256,16,128]{3,1,2,0:T(8,128)} copy(f32[16,256,16,128]{1,3,2,0:T(8,128)} %bitcast_add_fusion.1) | data formatting | bytes 67108864 | tf_op jit(solution)/shard_map/while | solution.py:95
  540.0 15.3 copy.51
  555.3 0.0 copy-done
  555.3 0.0 copy-done.2
  555.3 1374.1 %while.23 = (s32[]{:T(128)}, bf16[16,256,16,128]{3,1,2,0:T(8,128)(2,1)}, bf16[16,256,16,128]{3,1,2,0:T(8,128)(2,1)}, f32[16,16,256]{2,1,0:T(8,128)S(1)}, f32[16,...) while((s32[]{:T(128)}, ...), condition=%wide.region_9.10_spmd, body=%wide.region_3.9_spmd.sunk | while | flops 8757903360 | bytes 524288576 | solution.py:95
  555.3 0.5 collective-permute-start
  555.8 2.6 collective-permute-start.1
  558.4 180.3 %collective-permute-done = bf16[16,256,16,128]{3,1,2,0:T(8,128)(2,1)} collective-permute-done((bf16[16,256,16,128]{3,1,2,0:T(8,128)(2,1)}, bf16[16,256,16,128]{3,1,2,0:T(8,128)(2,1)}, u32[]{:S(2)}, u32[]{:S(2)}) %collective-permute-start) | collective-permute-done | bytes 16777248 | tf_op jit(solution)/shard_map/while/body/eval_jaxpr/ppermute | solution.py:83
  738.7 179.8 %collective-permute-done.1 = bf16[16,256,16,128]{3,1,2,0:T(8,128)(2,1)} collective-permute-done((bf16[16,256,16,128]{3,1,2,0:T(8,128)(2,1)}, bf16[16,256,16,128]{3,1,2,0:T(8,128)(2,1)}, u32[]{:S(2)}, u32[]{:S(2)}) %collective-permute-start.1) | collective-permute-done | bytes 16777248 | tf_op jit(solution)/shard_map/while/body/eval_jaxpr/ppermute | solution.py:84
  918.5 14.0 copy.75
  932.5 14.0 copy.76
  946.6 103.3 %collective-permute-start = (bf16[16,256,16,128]{3,1,2,0:T(8,128)(2,1)}, bf16[16,256,16,128]{3,1,2,0:T(8,128)(2,1)}, u32[]{:S(2)}, u32[]{:S(2)}) collective-permute-start(bf16[16,256,16,128]{3,1,2,0:T(8,128)(2,1)} %get-tuple-element.350), channel_id=1, source_target_pairs={{0,1},{1,2},{2,3},{3,0},{4,5},{5,6},{6,7},{7,4},{8,9},{9,10},{10,1... | collective-permute-start | bytes 50331656 | tf_op jit(solution)/shard_map/while/body/eval_jaxpr/ppermute | solution.py:83
  1049.8 2.5 collective-permute-start.1
  1052.3 177.8 %collective-permute-done = bf16[16,256,16,128]{3,1,2,0:T(8,128)(2,1)} collective-permute-done((bf16[16,256,16,128]{3,1,2,0:T(8,128)(2,1)}, bf16[16,256,16,128]{3,1,2,0:T(8,128)(2,1)}, u32[]{:S(2)}, u32[]{:S(2)}) %collective-permute-start) | collective-permute-done | bytes 16777248 | tf_op jit(solution)/shard_map/while/body/eval_jaxpr/ppermute | solution.py:83
  1230.2 179.8 %collective-permute-done.1 = bf16[16,256,16,128]{3,1,2,0:T(8,128)(2,1)} collective-permute-done((bf16[16,256,16,128]{3,1,2,0:T(8,128)(2,1)}, bf16[16,256,16,128]{3,1,2,0:T(8,128)(2,1)}, u32[]{:S(2)}, u32[]{:S(2)}) %collective-permute-start.1) | collective-permute-done | bytes 16777248 | tf_op jit(solution)/shard_map/while/body/eval_jaxpr/ppermute | solution.py:84
  1409.9 14.0 copy.75
  1423.9 14.0 copy.76
  1438.0 2.4 collective-permute-start
  1440.4 105.9 %collective-permute-start.1 = (bf16[16,256,16,128]{3,1,2,0:T(8,128)(2,1)}, bf16[16,256,16,128]{3,1,2,0:T(8,128)(2,1)}, u32[]{:S(2)}, u32[]{:S(2)}) collective-permute-start(bf16[16,256,16,128]{3,1,2,0:T(8,128)(2,1)} %get-tuple-element.351), channel_id=1, source_target_pairs={{0,1},{1,2},{2,3},{3,0},{4,5},{5,6},{6,7},{7,4},{8,9},{9,10},{10,1... | collective-permute-start | bytes 50331656 | tf_op jit(solution)/shard_map/while/body/eval_jaxpr/ppermute | solution.py:84
  1546.2 175.3 %collective-permute-done = bf16[16,256,16,128]{3,1,2,0:T(8,128)(2,1)} collective-permute-done((bf16[16,256,16,128]{3,1,2,0:T(8,128)(2,1)}, bf16[16,256,16,128]{3,1,2,0:T(8,128)(2,1)}, u32[]{:S(2)}, u32[]{:S(2)}) %collective-permute-start) | collective-permute-done | bytes 16777248 | tf_op jit(solution)/shard_map/while/body/eval_jaxpr/ppermute | solution.py:83
  1721.6 179.8 %collective-permute-done.1 = bf16[16,256,16,128]{3,1,2,0:T(8,128)(2,1)} collective-permute-done((bf16[16,256,16,128]{3,1,2,0:T(8,128)(2,1)}, bf16[16,256,16,128]{3,1,2,0:T(8,128)(2,1)}, u32[]{:S(2)}, u32[]{:S(2)}) %collective-permute-start.1) | collective-permute-done | bytes 16777248 | tf_op jit(solution)/shard_map/while/body/eval_jaxpr/ppermute | solution.py:84
  1901.4 14.0 copy.75
  1915.3 14.0 copy.76
  1929.4 32.0 %copy.28 = f32[16,256,16,128]{1,3,2,0:T(8,128)} copy(f32[16,256,16,128]{3,1,2,0:T(8,128)} %get-tuple-element.201) | data formatting | bytes 67108864 | tf_op jit(solution)/shard_map/while | solution.py:95
  1961.4 14.3 divide_convert_fusion
  1975.7 0.0 slice-done.2
  1975.7 0.0 slice-done.3
  1975.7 39.9 %convolution_convert_fusion = bf16[16,256,2048]{2,1,0:T(8,128)(2,1)} fusion(bf16[16,256,2048]{1,2,0:T(8,128)(2,1)S(1)} %bitcast.55, bf16[2048,2048]{1,0:T(8,128)(2,1)S(1)} %bitcast.61), kind=kOutput, calls=%fused_computation.36 | convolution fusion | flops 34368126976 | bytes 41943040 | tf_op jit(solution)/shard_map/dot_general | solution.py:61
  2015.6 141.2 %pmax.7 = f32[16]{0:T(128)S(1)} all-reduce(f32[16]{0:T(128)S(1)} %get-tuple-element.203), channel_id=1, replica_groups=mesh['dp'=8,'cp'=4] {'dp','cp'}, use_global_device_ids=true, to_apply=%region_10.11 | all-reduce | flops 16 | bytes 128 | tf_op jit(solution)/shard_map/pmax | solution.py:97
  2156.9 0.1 broadcast_bitcast_fusion
  2156.9 12.5 multiply_convert_fusion
  (18 shorter events, 0.1 us)
Async XLA Ops:
  43.8 72.4 %slice-start = ((s8[8388608]{0:T(1024)(128)(4,1)}), s8[4194304]{0:T(1024)(128)(4,1)S(1)}, s32[]{:S(2)}) async-start(s8[8388608]{0:T(1024)(128)(4,1)} %bitcast.58), calls=%async_computation | async-start | bytes 8388608
  71.5 44.7 %slice-start.1 = ((s8[8388608]{0:T(1024)(128)(4,1)}), s8[4194304]{0:T(1024)(128)(4,1)S(1)}, s32[]{:S(2)}) async-start(s8[8388608]{0:T(1024)(128)(4,1)} %bitcast.58), calls=%async_computation.1 | async-start | bytes 8388608
  184.8 44.7 %copy-start.1 = (s32[256]{0:T(256)S(1)}, s32[256]{0:T(256)}, u32[]{:S(2)}) copy-start(s32[256]{0:T(256)} %param.11) | copy-start | bytes 3076
  540.0 15.3 copy-start
  540.0 15.3 copy-start.2
  555.3 183.5 %collective-permute-start = (bf16[16,256,16,128]{3,1,2,0:T(8,128)(2,1)}, bf16[16,256,16,128]{3,1,2,0:T(8,128)(2,1)}, u32[]{:S(2)}, u32[]{:S(2)}) collective-permute-start(bf16[16,256,16,128]{3,1,2,0:T(8,128)(2,1)} %get-tuple-element.350), channel_id=1, source_target_pairs={{0,1},{1,2},{2,3},{3,0},{4,5},{5,6},{6,7},{7,4},{8,9},{9,10},{10,1... | collective-permute-start | bytes 50331656 | tf_op jit(solution)/shard_map/while/body/eval_jaxpr/ppermute | solution.py:83
  555.8 362.7 %collective-permute-start.1 = (bf16[16,256,16,128]{3,1,2,0:T(8,128)(2,1)}, bf16[16,256,16,128]{3,1,2,0:T(8,128)(2,1)}, u32[]{:S(2)}, u32[]{:S(2)}) collective-permute-start(bf16[16,256,16,128]{3,1,2,0:T(8,128)(2,1)} %get-tuple-element.351), channel_id=1, source_target_pairs={{0,1},{1,2},{2,3},{3,0},{4,5},{5,6},{6,7},{7,4},{8,9},{9,10},{10,1... | collective-permute-start | bytes 50331656 | tf_op jit(solution)/shard_map/while/body/eval_jaxpr/ppermute | solution.py:84
  946.6 283.6 %collective-permute-start = (bf16[16,256,16,128]{3,1,2,0:T(8,128)(2,1)}, bf16[16,256,16,128]{3,1,2,0:T(8,128)(2,1)}, u32[]{:S(2)}, u32[]{:S(2)}) collective-permute-start(bf16[16,256,16,128]{3,1,2,0:T(8,128)(2,1)} %get-tuple-element.350), channel_id=1, source_target_pairs={{0,1},{1,2},{2,3},{3,0},{4,5},{5,6},{6,7},{7,4},{8,9},{9,10},{10,1... | collective-permute-start | bytes 50331656 | tf_op jit(solution)/shard_map/while/body/eval_jaxpr/ppermute | solution.py:83
  1049.8 360.1 %collective-permute-start.1 = (bf16[16,256,16,128]{3,1,2,0:T(8,128)(2,1)}, bf16[16,256,16,128]{3,1,2,0:T(8,128)(2,1)}, u32[]{:S(2)}, u32[]{:S(2)}) collective-permute-start(bf16[16,256,16,128]{3,1,2,0:T(8,128)(2,1)} %get-tuple-element.351), channel_id=1, source_target_pairs={{0,1},{1,2},{2,3},{3,0},{4,5},{5,6},{6,7},{7,4},{8,9},{9,10},{10,1... | collective-permute-start | bytes 50331656 | tf_op jit(solution)/shard_map/while/body/eval_jaxpr/ppermute | solution.py:84
  1438.0 283.6 %collective-permute-start = (bf16[16,256,16,128]{3,1,2,0:T(8,128)(2,1)}, bf16[16,256,16,128]{3,1,2,0:T(8,128)(2,1)}, u32[]{:S(2)}, u32[]{:S(2)}) collective-permute-start(bf16[16,256,16,128]{3,1,2,0:T(8,128)(2,1)} %get-tuple-element.350), channel_id=1, source_target_pairs={{0,1},{1,2},{2,3},{3,0},{4,5},{5,6},{6,7},{7,4},{8,9},{9,10},{10,1... | collective-permute-start | bytes 50331656 | tf_op jit(solution)/shard_map/while/body/eval_jaxpr/ppermute | solution.py:83
  1440.4 461.0 %collective-permute-start.1 = (bf16[16,256,16,128]{3,1,2,0:T(8,128)(2,1)}, bf16[16,256,16,128]{3,1,2,0:T(8,128)(2,1)}, u32[]{:S(2)}, u32[]{:S(2)}) collective-permute-start(bf16[16,256,16,128]{3,1,2,0:T(8,128)(2,1)} %get-tuple-element.351), channel_id=1, source_target_pairs={{0,1},{1,2},{2,3},{3,0},{4,5},{5,6},{6,7},{7,4},{8,9},{9,10},{10,1... | collective-permute-start | bytes 50331656 | tf_op jit(solution)/shard_map/while/body/eval_jaxpr/ppermute | solution.py:84
  1961.4 14.3 slice-start.2
  1961.4 14.3 slice-start.3
  2156.9 12.6 copy-start.3
where the time goes:
time: 2180 us; the launch traced here: 2170 us
  waiting for transfers between devices  1070 us (49%)
  local copies, waits for them, and re-layouts  308 us (14%)
  matrix products  242 us (11%)
  starting transfers between devices  217 us (10%)
  other arithmetic  187 us (9%)
  blocking collectives  141 us (6%)
    ppermute x3, waiting for transfers between devices, step(): v_blk = lax.ppermute(v_blk, 'cp', shift_pairs)  539 us
    ppermute x3, waiting for transfers between devices, step(): k_blk = lax.ppermute(k_blk, 'cp', shift_pairs)  534 us
    pmax x1, blocking collectives, device_body(): head_max = lax.pmax(head_max, ('dp', 'cp'))  141 us
    ppermute x3, starting transfers between devices, step(): v_blk = lax.ppermute(v_blk, 'cp', shift_pairs)  111 us
    ppermute x3, starting transfers between devices, step(): k_blk = lax.ppermute(k_blk, 'cp', shift_pairs)  106 us
    another operation x1, other arithmetic  96.4 us
    slice x2, local copies, waits for them, and re-layouts, rope_rotate(): lead_half = tensor[..., :half_dim]  89.4 us
    while x6, local copies, waits for them, and re-layouts  84.1 us
  transfers between devices with their start and end apart: 6, of which 6 were waited for; matrix products, arithmetic and copies ran while one was open for 0% of the time, Pallas kernels for 0%

commit v1 on v0

v1 whole, which is shorter than its diff:
```python
import functools

import jax
import jax.numpy as jnp
from jax import lax
from jax.experimental import pallas as pl
from jax.experimental.pallas import tpu as pltpu
from jax.sharding import PartitionSpec as P


HEAD_DIM = 128
TAU_CLIP = 100.0
ROPE_THETA = 50000.0
GROUP = 2 * HEAD_DIM
STEP_ROWS = 2
NEG = -1e30


def rope_tables(pos_ids):
    half_dim = HEAD_DIM // 2
    inv_freq = jnp.float32(ROPE_THETA) ** (-jnp.arange(half_dim, dtype=jnp.float32) * (2.0 / HEAD_DIM))
    angle = pos_ids.astype(jnp.float32)[:, None] * inv_freq[None, :]
    cos_t, sin_t = jnp.cos(angle), jnp.sin(angle)
    return jnp.concatenate([cos_t, cos_t], axis=-1), jnp.concatenate([-sin_t, sin_t], axis=-1)


def rows_kernel(whole, chained, piece, meta, x_own, x_sib, x_str, x_crs, w_q, w_k, w_v, w_o, cos_t, sin_t, *refs):
    if chained:
        refs = refs[1:]
    if whole:
        o_keep, o_send, o_str, o_crs, top, q_scr, k_scr, v_scr, att, wo_scr, sem = refs
    else:
        o_keep, o_send, top, q_scr, k_scr, v_scr, att, wo_scr, sem = refs
    step = pl.program_id(0)
    n_steps = pl.num_programs(0)
    chip, core = meta[0], meta[1]
    rows = STEP_ROWS
    local_off = 0 if whole else 2 * piece
    remote_off = 2 * piece if whole else 0
    scale = HEAD_DIM ** -0.5

    def wo_copy():
        return pltpu.make_async_copy(w_o, wo_scr, sem)

    def project(x_ref, slot, base, piece_id, with_q):
        x2 = x_ref[...].reshape(rows * piece, x_ref.shape[2])
        at = pl.multiple_of(base + slot * piece, piece)
        pos = pl.ds(pl.multiple_of(piece_id * piece, piece), piece)
        cos_p, sin_p = cos_t[pos, :], sin_t[pos, :]

        def rotated(w_ref, dst):
            t = jnp.dot(x2, w_ref[...], preferred_element_type=jnp.float32)
            for r in range(rows):
                for h in range(2):
                    th = t[r * piece:(r + 1) * piece, h * HEAD_DIM:(h + 1) * HEAD_DIM]
                    th = th * cos_p + pltpu.roll(th, HEAD_DIM // 2, axis=1) * sin_p
                    dst[r, pl.ds(at, piece), h * HEAD_DIM:(h + 1) * HEAD_DIM] = th.astype(jnp.bfloat16)

        if with_q:
            rotated(w_q, q_scr)
        rotated(w_k, k_scr)
        v = jnp.dot(x2, w_v[...], preferred_element_type=jnp.float32).astype(jnp.bfloat16)
        for r in range(rows):
            v_scr[r, pl.ds(at, piece), :] = v[r * piece:(r + 1) * piece]

    def attend(q_blocks, key_start, att_base):
        causal = lax.broadcasted_iota(jnp.int32, (piece, piece), 0) >= lax.broadcasted_iota(jnp.int32, (piece, piece), 1)
        nt = (((1,), (1,)), ((), ()))
        for h in range(2):
            cols = slice(h * HEAD_DIM, (h + 1) * HEAD_DIM)
            best = None
            for r in range(rows):
                for q_at in q_blocks:
                    q = q_scr[r, q_at:q_at + piece, cols]
                    s_diag = lax.dot_general(q, k_scr[r, q_at:q_at + piece, cols], nt, preferred_element_type=jnp.float32)
                    s_diag = jnp.where(causal, s_diag, NEG)
                    m = jnp.max(s_diag, axis=1, keepdims=True)
                    if q_at > key_start:
                        s_past = lax.dot_general(q, k_scr[r, key_start:q_at, cols], nt, preferred_element_type=jnp.float32)
                        m = jnp.maximum(m, jnp.max(s_past, axis=1, keepdims=True))
                    p_diag = jnp.exp((s_diag - m) * scale)
                    total = jnp.sum(p_diag, axis=1, keepdims=True)
                    acc = jnp.dot(p_diag.astype(jnp.bfloat16), v_scr[r, q_at:q_at + piece, cols], preferred_element_type=jnp.float32)
                    if q_at > key_start:
                        p_past = jnp.exp((s_past - m) * scale)
                        total = total + jnp.sum(p_past, axis=1, keepdims=True)
                        acc = acc + jnp.dot(p_past.astype(jnp.bfloat16), v_scr[r, key_start:q_at, cols], preferred_element_type=jnp.float32)
                    slot = q_at // piece - att_base
                    col = pl.multiple_of(step * GROUP + h * HEAD_DIM, HEAD_DIM)
                    att[slot, r * piece:(r + 1) * piece, pl.ds(col, HEAD_DIM)] = (acc / total).astype(jnp.bfloat16)
                    m_top = jnp.max(m)
                    best = m_top if best is None else jnp.maximum(best, m_top)
            top[0, h, :] = jnp.full((top.shape[2],), best * scale, jnp.float32)

    def project_out(slot, o_ref):
        width = wo_scr.shape[1]
        cut = min(512, width)
        for n in range(0, width, cut):
            o = jnp.dot(att[slot], wo_scr[:, n:n + cut], preferred_element_type=jnp.float32).astype(jnp.bfloat16)
            o_ref[:, :, n:n + cut] = o.reshape(rows, piece, cut)

    top[...] = jnp.full(top.shape, -jnp.inf, jnp.float32)

    def work():
        @pl.when(step == 0)
        def _():
            wo_copy().start()

        project(x_own, core, local_off, 2 * chip + core, True)
        project(x_sib, 1 - core, local_off, 2 * chip + 1 - core, True)
        if whole:
            project(x_str, core, remote_off, 2 * (1 - chip) + core, True)
            project(x_crs, 1 - core, remote_off, 2 * (1 - chip) + 1 - core, True)
            attend([j * piece for j in range(4)], 0, 0)
        else:
            @pl.when(chip == 1)
            def _():
                project(x_str, core, remote_off, core, False)
                project(x_crs, 1 - core, remote_off, 1 - core, False)
                attend([2 * piece, 3 * piece], 0, 2)

            @pl.when(chip == 0)
            def _():
                attend([2 * piece, 3 * piece], 2 * piece, 2)

        @pl.when(step == n_steps - 1)
        def _():
            wo_copy().wait()
            project_out(core, o_keep)
            project_out(1 - core, o_send)
            if whole:
                project_out(2 + core, o_str)
                project_out(3 - core, o_crs)

    if whole:
        pl.when(chip == 0)(work)
    else:
        work()


def rows_call(whole, block, out, meta, hidden, sib, straight, cross, w_q, w_k, w_v, w_o, cos_t, sin_t):
    rows, piece, d_model = STEP_ROWS, hidden.shape[1], hidden.shape[2]
    width = w_q.shape[1]
    n_steps = width // GROUP
    n_blocks = hidden.shape[0] // rows
    once = pl.Buffered(1)
    x_block = (rows, piece, d_model)
    x_spec = pl.BlockSpec(x_block, lambda g, m: (0, 0, 0), pipeline_mode=once)
    own_spec = pl.BlockSpec(x_block, lambda g, m: (m[1] * (n_blocks // 2) + block, 0, 0), pipeline_mode=once)
    w_spec = pl.BlockSpec((d_model, GROUP), lambda g, m: (0, g))
    t_spec = pl.BlockSpec(cos_t.shape, lambda g, m: (0, 0), pipeline_mode=once)
    n_out = 4 if whole else 2
    out_shape = [jax.ShapeDtypeStruct(x_block, jnp.bfloat16)] * n_out + [jax.ShapeDtypeStruct((n_steps, 8, 128), jnp.float32)]
    out_specs = [x_spec] * n_out + [pl.BlockSpec((1, 8, 128), lambda g, m: (g, 0, 0))]
    if not whole:
        out_shape[0] = jax.ShapeDtypeStruct(hidden.shape, jnp.bfloat16)
        out_specs[0] = own_spec
    any_spec = pl.BlockSpec(memory_space=pl.ANY)
    chained = out is not None
    tokens = rows * 4 * piece
    flops = tokens * d_model * width * (8 if whole else 6) + 4 * rows * width * 10 * piece * piece
    return pl.pallas_call(
        functools.partial(rows_kernel, whole, chained, piece),
        out_shape=out_shape,
        grid_spec=pltpu.PrefetchScalarGridSpec(
            num_scalar_prefetch=1,
            grid=(n_steps,),
            in_specs=[own_spec, x_spec, x_spec, x_spec, w_spec, w_spec, w_spec, any_spec, t_spec, t_spec] + [any_spec] * chained,
            out_specs=out_specs,
            scratch_shapes=[
                pltpu.VMEM((rows, 4 * piece, GROUP), jnp.bfloat16),
                pltpu.VMEM((rows, 4 * piece, GROUP), jnp.bfloat16),
                pltpu.VMEM((rows, 4 * piece, GROUP), jnp.bfloat16),
                pltpu.VMEM((n_out, rows * piece, width), jnp.bfloat16),
                pltpu.VMEM((width, d_model), jnp.bfloat16),
                pltpu.SemaphoreType.DMA,
            ],
        ),
        compiler_params=pltpu.CompilerParams(dimension_semantics=("arbitrary",), vmem_limit_bytes=66_000_000),
        cost_estimate=pl.CostEstimate(flops=flops, bytes_accessed=60_000_000, transcendentals=0),
        input_output_aliases={11: 0} if chained else {},
        name="whole_rows" if whole else "half_rows",
    )(meta, hidden, sib, straight, cross, w_q, w_k, w_v, w_o, cos_t, sin_t, *([out] if chained else []))


def clip_weights(head_max, w_q, w_k):
    factor = jnp.where(head_max > TAU_CLIP, jnp.sqrt(TAU_CLIP / head_max), 1.0)
    col_factor = jnp.repeat(factor, HEAD_DIM)[None, :]
    return (w_q.astype(jnp.float32) * col_factor).astype(jnp.bfloat16), (w_k.astype(jnp.float32) * col_factor).astype(jnp.bfloat16)


def solution(mesh):
    in_chip = [(0, 1), (1, 0), (2, 3), (3, 2)]
    up_straight, up_cross = [(0, 2), (1, 3)], [(0, 3), (1, 2)]
    down_straight, down_cross = [(2, 0), (3, 1)], [(2, 1), (3, 0)]

    def layer(hidden, pos_ids, w_q, w_k, w_v, w_o):
        rank = lax.axis_index("cp")
        chip, core = rank // 2, rank % 2
        meta = jnp.stack([chip, core]).astype(jnp.int32)
        batch_n = hidden.shape[0]
        half = batch_n // 2
        n_calls = half // STEP_ROWS

        def rows_of(array, which, block):
            return lax.dynamic_slice_in_dim(array, which * half + block * STEP_ROWS, STEP_ROWS, axis=0)

        def send(x, pairs):
            return lax.ppermute(x, "cp", pairs)

        last = n_calls - 1
        order = list(range(n_calls))
        mine, other = [rows_of(hidden, core, 0)], [rows_of(hidden, 1 - core, 0)]
        later, mine[0], other[0] = lax.optimization_barrier((hidden, mine[0], other[0]))
        mine += [rows_of(later, core, b) for b in order[1:]]
        other += [rows_of(later, 1 - core, b) for b in order[1:]]
        straight = [send(mine[b], down_straight if b == last else up_straight) for b in order]
        cross = [send(other[b], down_cross if b == last else up_cross) for b in order]
        sib = [send(other[b], in_chip) for b in order]
        cos_t, sin_t = rope_tables(lax.all_gather(pos_ids, "cp", tiled=True))

        def call(b, out):
            return rows_call(b == last, b, out, meta, hidden, sib[b], straight[b], cross[b], w_q, w_k, w_v, w_o, cos_t, sin_t)

        keep, give, ret_straight, ret_cross, top = call(last, None)
        tops = [top]
        give = send(give, in_chip)
        keep = jnp.where(chip == 1, send(ret_straight, up_straight), keep)
        give = jnp.where(chip == 1, send(ret_cross, up_cross), give)
        out, swapped = None, []
        for b in order[:last]:
            out, swap, top = call(b, out)
            tops.append(top)
            swapped.append(send(swap, in_chip))
        tops = [top[:, :2, 0].reshape(-1) for top in tops]
        for b in order:
            where = (1 - core) * half + b * STEP_ROWS
            out = lax.dynamic_update_slice_in_dim(out, give if b == last else swapped[b], where, axis=0)
        out = lax.dynamic_update_slice_in_dim(out, keep, core * half + last * STEP_ROWS, axis=0)
        head_max = functools.reduce(jnp.maximum, tops)
        head_max = lax.pmax(head_max, ("dp", "cp"))
        w_q_new, w_k_new = clip_weights(head_max, w_q, w_k)
        return out, head_max, w_q_new, w_k_new

    return jax.shard_map(
        layer,
        mesh=mesh,
        in_specs=(P("dp", "cp", None), P("cp"), P(None, None), P(None, None), P(None, None), P(None, None)),
        out_specs=(P("dp", "cp", None), P(None), P(None, None), P(None, None)),
        check_vma=False,
    )
```

time: 2180 us -> 680 us (0.31)
  waiting for transfers between devices: 1070 us -> 47.1 us
  Pallas kernels: 0 us -> 341 us
  local copies, waits for them, and re-layouts: 308 us -> 22.9 us
  matrix products: 242 us -> 0 us
  starting transfers between devices: 217 us -> 42.3 us
  other arithmetic: 187 us -> 23.2 us
  blocking collectives: 141 us -> 199 us
    ppermute x6 -> x18, waiting for transfers between devices: 1070 us -> 47.1 us  [send(): return lax.ppermute(x, 'cp', pairs)]
    pallas_call x0 -> x4, Pallas kernels: none -> 341 us  [rows_call(): pl.pallas_call(functools.partial(rows_kernel, whole, chained, piece), out...]
    dot_general x6 -> x0, matrix products: 242 us -> none  [the longest x1 43.4 us: attend_block(): jnp.einsum('bhqk,bkhd->bqhd', prob_w.astype(jnp.bfloat16), v_blk, preferr...]
    ppermute x6 -> x18, starting transfers between devices: 217 us -> 42.3 us  [send(): return lax.ppermute(x, 'cp', pairs)]
    while x8 -> x0, local copies, waits for them, and re-layouts: 148 us -> none
    all_gather x0 -> x1, blocking collectives: none -> 120 us  [layer(): cos_t, sin_t = rope_tables(lax.all_gather(pos_ids, 'cp', tiled=True))]
    another operation x2 -> x1, other arithmetic: 97.1 us -> 0.67 us  [layer(): meta = jnp.stack([chip, core]).astype(jnp.int32)]
    slice x2 -> x0, local copies, waits for them, and re-layouts: 89.4 us -> none  [rope_rotate(): lead_half = tensor[..., :half_dim]]
  transfers between devices with their start and end apart: 6 -> 18, of which waited for: 6 -> 3; matrix products, arithmetic and copies ran while one was open for 0% -> 6% of each run, Pallas kernels for 0% -> 50%
where the time goes in v1:
time: 680 us; the launch traced here: 676 us
  Pallas kernels  341 us (50%)
  blocking collectives  199 us (29%)
  waiting for transfers between devices  47.1 us (7%)
  starting transfers between devices  42.3 us (6%)
  other arithmetic  23.2 us (3%)
  local copies, waits for them, and re-layouts  22.9 us (3%)
    pallas_call x4, Pallas kernels, rows_call(): pl.pallas_call(functools.partial(rows_kernel, whole, chained, piece), out...  341 us
    all_gather x1, blocking collectives, layer(): cos_t, sin_t = rope_tables(lax.all_gather(pos_ids, 'cp', tiled=True))  120 us
    pmax x1, blocking collectives, layer(): head_max = lax.pmax(head_max, ('dp', 'cp'))  79.6 us
    ppermute x18, waiting for transfers between devices, send(): return lax.ppermute(x, 'cp', pairs)  47.1 us
    ppermute x18, starting transfers between devices, send(): return lax.ppermute(x, 'cp', pairs)  42.3 us
  transfers between devices with their start and end apart: 18, of which 3 were waited for; matrix products, arithmetic and copies ran while one was open for 6% of the time, Pallas kernels for 50%

profile of v1, /device:TPU:0, one launch (start us, length us, event | category | flops | bytes accessed | tf_op | source)
XLA Modules:
  0.0 676.4 jit_solution(18095126116263499153)
XLA Ops:
  0.7 4.0 constant_dynamic-slice_fusion.6
  4.7 0.5 collective-permute-start.6
  5.1 5.7 collective-permute-start.7
  10.9 2.6 collective-permute-start.8
  13.5 9.3 %constant_dynamic-slice_fusion = (bf16[2,256,2048]{2,1,0:T(8,128)(2,1)}, bf16[2,256,2048]{2,1,0:T(8,128)(2,1)}, bf16[2,256,2048]{2,1,0:T(8,128)(2,1)}, bf16[2,25...) fusion(bf16[16,256,2048]{2,1,0:T(8,128)(2,1)} %x_own.7, s32[]{:T(128)S(6)} %select_n.66, ...), kind=kLoop, calls=%fused_computation.11 | loop fusion | bytes 25165848 | tf_op jit(solution)/shard_map/dynamic_slice | solution.py:206
  22.7 0.3 collective-permute-start
  23.0 2.6 collective-permute-start.2
  25.6 119.6 %all-gather = s32[4,1,256]{2,1,0:T(1,128)S(1)} all-gather(s32[1,1,256]{2,1,0:T(1,128)S(1)} %bitcast.7), channel_id=1, replica_groups=mesh['dp'=8,'cp'=4] {'cp'}, dimensions={0}, use_global_device_ids=true | all-gather | bytes 5120 | tf_op jit(solution)/shard_map/all_gather | solution.py:220
  145.3 0.7 pad_add_fusion.meta
  146.0 1.9 fusion
  147.9 1.3 pad_maximum_fusion
  149.2 0.0 collective-permute-done.6.x_sib
  149.2 0.0 collective-permute-start.3
  149.2 0.0 collective-permute-done.7.x_str
  149.2 6.6 collective-permute-start.5
  155.8 0.0 collective-permute-done.8.x_crs
  155.8 2.7 collective-permute-start.4
  158.5 65.7 %half_rows.3 = (bf16[16,256,2048]{2,1,0:T(8,128)(2,1)}, bf16[2,256,2048]{2,1,0:T(8,128)(2,1)}, f32[8,8,128]{2,1,0:T(8,128)}) custom-call(s32[2]{0:T(128)} %pad_add_fusion.meta, bf16[16,256,2048]{2,1,0:T(8,128)(2,1)} %x_own.7, bf16[2,256,2048]{2,1,0:T(8,128)(2,1)} %collective-permute-done.6.x_sib, bf16[2,256,2048]{2,1,0:T(8,128)(2,1)} %collective-permute-done.7.x_str, ...), custom_call_target="tpu_custom_call" | custom-call | flops 62277025792 | bytes 60000000 | tf_op jit(solution)/shard_map/half_rows/pallas_call | solution.py:162
  224.2 0.0 collective-permute-done.3.x_sib
  224.2 0.4 collective-permute-start.12
  224.6 20.8 %collective-permute-done.4.x_str = bf16[2,256,2048]{2,1,0:T(8,128)(2,1)} collective-permute-done((bf16[2,256,2048]{2,1,0:T(8,128)(2,1)}, bf16[2,256,2048]{2,1,0:T(8,128)(2,1)}, u32[]{:S(2)}, u32[]{:S(2)}) %collective-permute-start.4) | collective-permute-done | bytes 2097184 | tf_op jit(solution)/shard_map/ppermute | solution.py:209
  245.3 1.3 collective-permute-start.14
  246.6 11.8 %collective-permute-start.1 = (bf16[2,256,2048]{2,1,0:T(8,128)(2,1)}, bf16[2,256,2048]{2,1,0:T(8,128)(2,1)}, u32[]{:S(2)}, u32[]{:S(2)}) collective-permute-start(bf16[2,256,2048]{2,1,0:T(8,128)(2,1)} %get-tuple-element.42), channel_id=1, source_target_pairs={{0,2},{1,3},{4,6},{5,7},{8,10},{9,11},{12,14},{13,15},{16,18},{17,... | collective-permute-start | bytes 6291464 | tf_op jit(solution)/shard_map/ppermute | solution.py:209
  258.5 76.3 %half_rows.4 = (bf16[16,256,2048]{2,1,0:T(8,128)(2,1)}, bf16[2,256,2048]{2,1,0:T(8,128)(2,1)}, f32[8,8,128]{2,1,0:T(8,128)}) custom-call(s32[2]{0:T(128)} %pad_add_fusion.meta, bf16[16,256,2048]{2,1,0:T(8,128)(2,1)} %x_own.7, bf16[2,256,2048]{2,1,0:T(8,128)(2,1)} %collective-permute-done.3.x_sib, ...), custom_call_target="tpu_custom_call", output_to_operand_aliasing={{0}: (11, {})} | custom-call | flops 62277025792 | bytes 60000000 | tf_op jit(solution)/shard_map/half_rows/pallas_call | solution.py:162
  334.8 1.3 collective-permute-start.13
  336.1 0.0 collective-permute-done.1.x_str
  336.1 0.1 collective-permute-start.9
  336.2 0.0 collective-permute-done.2.x_crs
  336.2 0.4 collective-permute-start.10
  336.7 65.8 %half_rows.5 = (bf16[16,256,2048]{2,1,0:T(8,128)(2,1)}, bf16[2,256,2048]{2,1,0:T(8,128)(2,1)}, f32[8,8,128]{2,1,0:T(8,128)}) custom-call(s32[2]{0:T(128)} %pad_add_fusion.meta, bf16[16,256,2048]{2,1,0:T(8,128)(2,1)} %x_own.7, bf16[2,256,2048]{2,1,0:T(8,128)(2,1)} %collective-permute-done.x_sib, ...), custom_call_target="tpu_custom_call", output_to_operand_aliasing={{0}: (11, {})} | custom-call | flops 62277025792 | bytes 60000000 | tf_op jit(solution)/shard_map/half_rows/pallas_call | solution.py:162
  402.5 0.0 collective-permute-done.12.x_sib
  402.5 0.2 collective-permute-start.11
  402.7 9.3 %collective-permute-done.13.x_str = bf16[2,256,2048]{2,1,0:T(8,128)(2,1)} collective-permute-done((bf16[2,256,2048]{2,1,0:T(8,128)(2,1)}, bf16[2,256,2048]{2,1,0:T(8,128)(2,1)}, u32[]{:S(2)}, u32[]{:S(2)}) %collective-permute-start.13) | collective-permute-done | bytes 2097184 | tf_op jit(solution)/shard_map/ppermute | solution.py:209
  412.0 132.8 %whole_rows.1 = (bf16[2,256,2048]{2,1,0:T(8,128)(2,1)}, bf16[2,256,2048]{2,1,0:T(8,128)(2,1)}, bf16[2,256,2048]{2,1,0:T(8,128)(2,1)}, bf16[2,256,2048]{2,1,0:T(8,128)(2,1)}, f32[8,8,128]{2,1,0:T(8,128)}) custom-call(s32[2]{0:T(128)} %pad_add_fusion.meta, bf16[16,256,2048]{2,1,0:T(8,128)(2,1)} %x_own.7, bf16[2,256,2048]{2,1,0:T(8,128)(2,1)} %collective-permute-done.12.x_sib, ...), custom_call_target="tpu_custom_call" | custom-call | flops 79456894976 | bytes 60000000 | tf_op jit(solution)/shard_map/whole_rows/pallas_call | solution.py:162
  544.8 1.4 collective-permute-start.15
  546.2 0.9 maximum_reduce_fusion
  547.1 0.1 max.19
  547.2 0.0 collective-permute-start.16
  547.2 79.6 %pmax.7 = f32[16]{0:T(128)S(1)} all-reduce(f32[16]{0:T(128)S(1)} %max.19), channel_id=1, replica_groups=mesh['dp'=8,'cp'=4] {'dp','cp'}, use_global_device_ids=true, to_apply=%region_0.1 | all-reduce | flops 16 | bytes 128 | tf_op jit(solution)/shard_map/pmax | solution.py:241
  626.8 0.1 broadcast_bitcast_fusion
  626.9 4.3 collective-permute-start.17
  631.2 12.5 %multiply_convert_fusion = (bf16[2048,2048]{1,0:T(8,128)(2,1)}, bf16[2048,2048]{1,0:T(8,128)(2,1)}) fusion(bf16[2048,2048]{1,0:T(8,128)(2,1)} %w_k.7, f32[2048]{0:T(1024)S(1)} %broadcast_bitcast_fusion, bf16[2048,2048]{1,0:T(8,128)(2,1)} %w_q.7), kind=kLoop, calls=%fused_computation | loop fusion | flops 25165824 | bytes 33562624 | tf_op jit(solution)/shard_map/convert_element_type | solution.py:189
  643.7 3.2 constant_dynamic-update-slice_fusion.2
  646.8 3.2 constant_dynamic-update-slice_fusion.1
  650.0 3.2 constant_dynamic-update-slice_fusion
  653.1 3.8 select_dynamic-update-slice_fusion.1
  657.0 17.0 %collective-permute-done.17 = bf16[2,256,2048]{2,1,0:T(8,128)(2,1)S(1)} collective-permute-done((bf16[2,256,2048]{2,1,0:T(8,128)(2,1)}, bf16[2,256,2048]{2,1,0:T(8,128)(2,1)S(1)}, u32[]{:S(2)}, u32[]{:S(2)}) %collective-permute-start.17) | collective-permute-done | bytes 2097184 | tf_op jit(solution)/shard_map/ppermute | solution.py:209
  674.0 2.1 select_dynamic-update-slice_fusion
  (17 shorter events, 0.1 us)
Async XLA Ops:
  4.7 144.5 %collective-permute-start.6 = (bf16[2,256,2048]{2,1,0:T(8,128)(2,1)S(1)}, bf16[2,256,2048]{2,1,0:T(8,128)(2,1)}, u32[]{:S(2)}, u32[]{:S(2)}) collective-permute-start(bf16[2,256,2048]{2,1,0:T(8,128)(2,1)S(1)} %get-tuple-element.22), channel_id=1, source_target_pairs={{0,1},{1,0},{2,3},{3,2},{4,5},{5,4},{6,7},{7,6},{8,9},{9,8},{10,11... | collective-permute-start | bytes 6291464 | tf_op jit(solution)/shard_map/ppermute | solution.py:209
  5.1 144.1 %collective-permute-start.7 = (bf16[2,256,2048]{2,1,0:T(8,128)(2,1)}, bf16[2,256,2048]{2,1,0:T(8,128)(2,1)}, u32[]{:S(2)}, u32[]{:S(2)}) collective-permute-start(bf16[2,256,2048]{2,1,0:T(8,128)(2,1)} %get-tuple-element.23), channel_id=1, source_target_pairs={{0,2},{1,3},{4,6},{5,7},{8,10},{9,11},{12,14},{13,15},{16,18},{17,... | collective-permute-start | bytes 6291464 | tf_op jit(solution)/shard_map/ppermute | solution.py:209
  10.9 144.9 %collective-permute-start.8 = (bf16[2,256,2048]{2,1,0:T(8,128)(2,1)S(1)}, bf16[2,256,2048]{2,1,0:T(8,128)(2,1)}, u32[]{:S(2)}, u32[]{:S(2)}) collective-permute-start(bf16[2,256,2048]{2,1,0:T(8,128)(2,1)S(1)} %get-tuple-element.22), channel_id=1, source_target_pairs={{0,3},{1,2},{4,7},{5,6},{8,11},{9,10},{12,15},{13,14},{16,19},{17,... | collective-permute-start | bytes 6291464 | tf_op jit(solution)/shard_map/ppermute | solution.py:209
  13.5 12.2 %copy-start.1 = (s32[256]{0:T(256)S(1)}, s32[256]{0:T(256)}, u32[]{:S(2)}) copy-start(s32[256]{0:T(256)} %param.7) | copy-start | bytes 3076
  22.7 312.1 %collective-permute-start = (bf16[2,256,2048]{2,1,0:T(8,128)(2,1)}, bf16[2,256,2048]{2,1,0:T(8,128)(2,1)}, u32[]{:S(2)}, u32[]{:S(2)}) collective-permute-start(bf16[2,256,2048]{2,1,0:T(8,128)(2,1)} %get-tuple-element.43), channel_id=1, source_target_pairs={{0,1},{1,0},{2,3},{3,2},{4,5},{5,4},{6,7},{7,6},{8,9},{9,8},{10,11... | collective-permute-start | bytes 6291464 | tf_op jit(solution)/shard_map/ppermute | solution.py:209
  23.0 313.2 %collective-permute-start.2 = (bf16[2,256,2048]{2,1,0:T(8,128)(2,1)}, bf16[2,256,2048]{2,1,0:T(8,128)(2,1)}, u32[]{:S(2)}, u32[]{:S(2)}) collective-permute-start(bf16[2,256,2048]{2,1,0:T(8,128)(2,1)} %get-tuple-element.43), channel_id=1, source_target_pairs={{0,3},{1,2},{4,7},{5,6},{8,11},{9,10},{12,15},{13,14},{16,19},{17,... | collective-permute-start | bytes 6291464 | tf_op jit(solution)/shard_map/ppermute | solution.py:209
  149.2 75.0 %collective-permute-start.3 = (bf16[2,256,2048]{2,1,0:T(8,128)(2,1)}, bf16[2,256,2048]{2,1,0:T(8,128)(2,1)}, u32[]{:S(2)}, u32[]{:S(2)}) collective-permute-start(bf16[2,256,2048]{2,1,0:T(8,128)(2,1)} %get-tuple-element.41), channel_id=1, source_target_pairs={{0,1},{1,0},{2,3},{3,2},{4,5},{5,4},{6,7},{7,6},{8,9},{9,8},{10,11... | collective-permute-start | bytes 6291464 | tf_op jit(solution)/shard_map/ppermute | solution.py:209
  149.2 97.4 %collective-permute-start.5 = (bf16[2,256,2048]{2,1,0:T(8,128)(2,1)}, bf16[2,256,2048]{2,1,0:T(8,128)(2,1)}, u32[]{:S(2)}, u32[]{:S(2)}) collective-permute-start(bf16[2,256,2048]{2,1,0:T(8,128)(2,1)} %get-tuple-element.41), channel_id=1, source_target_pairs={{0,3},{1,2},{4,7},{5,6},{8,11},{9,10},{12,15},{13,14},{16,19},{17,... | collective-permute-start | bytes 6291464 | tf_op jit(solution)/shard_map/ppermute | solution.py:209
  155.8 89.5 %collective-permute-start.4 = (bf16[2,256,2048]{2,1,0:T(8,128)(2,1)}, bf16[2,256,2048]{2,1,0:T(8,128)(2,1)}, u32[]{:S(2)}, u32[]{:S(2)}) collective-permute-start(bf16[2,256,2048]{2,1,0:T(8,128)(2,1)} %get-tuple-element.40), channel_id=1, source_target_pairs={{0,2},{1,3},{4,6},{5,7},{8,10},{9,11},{12,14},{13,15},{16,18},{17,... | collective-permute-start | bytes 6291464 | tf_op jit(solution)/shard_map/ppermute | solution.py:209
  224.2 178.4 %collective-permute-start.12 = (bf16[2,256,2048]{2,1,0:T(8,128)(2,1)}, bf16[2,256,2048]{2,1,0:T(8,128)(2,1)}, u32[]{:S(2)}, u32[]{:S(2)}) collective-permute-start(bf16[2,256,2048]{2,1,0:T(8,128)(2,1)} %get-tuple-element.39), channel_id=1, source_target_pairs={{0,1},{1,0},{2,3},{3,2},{4,5},{5,4},{6,7},{7,6},{8,9},{9,8},{10,11... | collective-permute-start | bytes 6291464 | tf_op jit(solution)/shard_map/ppermute | solution.py:209
  245.3 166.6 %collective-permute-start.14 = (bf16[2,256,2048]{2,1,0:T(8,128)(2,1)}, bf16[2,256,2048]{2,1,0:T(8,128)(2,1)}, u32[]{:S(2)}, u32[]{:S(2)}) collective-permute-start(bf16[2,256,2048]{2,1,0:T(8,128)(2,1)} %get-tuple-element.39), channel_id=1, source_target_pairs={{2,1},{3,0},{6,5},{7,4},{10,9},{11,8},{14,13},{15,12},{18,17},{19,... | collective-permute-start | bytes 6291464 | tf_op jit(solution)/shard_map/ppermute | solution.py:209
  246.6 89.5 %collective-permute-start.1 = (bf16[2,256,2048]{2,1,0:T(8,128)(2,1)}, bf16[2,256,2048]{2,1,0:T(8,128)(2,1)}, u32[]{:S(2)}, u32[]{:S(2)}) collective-permute-start(bf16[2,256,2048]{2,1,0:T(8,128)(2,1)} %get-tuple-element.42), channel_id=1, source_target_pairs={{0,2},{1,3},{4,6},{5,7},{8,10},{9,11},{12,14},{13,15},{16,18},{17,... | collective-permute-start | bytes 6291464 | tf_op jit(solution)/shard_map/ppermute | solution.py:209
  334.8 77.2 %collective-permute-start.13 = (bf16[2,256,2048]{2,1,0:T(8,128)(2,1)}, bf16[2,256,2048]{2,1,0:T(8,128)(2,1)}, u32[]{:S(2)}, u32[]{:S(2)}) collective-permute-start(bf16[2,256,2048]{2,1,0:T(8,128)(2,1)} %get-tuple-element.38), channel_id=1, source_target_pairs={{2,0},{3,1},{6,4},{7,5},{10,8},{11,9},{14,12},{15,13},{18,16},{19,... | collective-permute-start | bytes 6291464 | tf_op jit(solution)/shard_map/ppermute | solution.py:209
  336.1 290.8 %collective-permute-start.9 = (bf16[2,256,2048]{2,1,0:T(8,128)(2,1)}, bf16[2,256,2048]{2,1,0:T(8,128)(2,1)}, u32[]{:S(2)}, u32[]{:S(2)}) collective-permute-start(bf16[2,256,2048]{2,1,0:T(8,128)(2,1)} %get-tuple-element.27), channel_id=1, source_target_pairs={{0,1},{1,0},{2,3},{3,2},{4,5},{5,4},{6,7},{7,6},{8,9},{9,8},{10,11... | collective-permute-start | bytes 6291464 | tf_op jit(solution)/shard_map/ppermute | solution.py:209
  336.2 310.6 %collective-permute-start.10 = (bf16[2,256,2048]{2,1,0:T(8,128)(2,1)}, bf16[2,256,2048]{2,1,0:T(8,128)(2,1)}, u32[]{:S(2)}, u32[]{:S(2)}) collective-permute-start(bf16[2,256,2048]{2,1,0:T(8,128)(2,1)} %get-tuple-element.28), channel_id=1, source_target_pairs={{0,1},{1,0},{2,3},{3,2},{4,5},{5,4},{6,7},{7,6},{8,9},{9,8},{10,11... | collective-permute-start | bytes 6291464 | tf_op jit(solution)/shard_map/ppermute | solution.py:209
  402.5 247.4 %collective-permute-start.11 = (bf16[2,256,2048]{2,1,0:T(8,128)(2,1)}, bf16[2,256,2048]{2,1,0:T(8,128)(2,1)}, u32[]{:S(2)}, u32[]{:S(2)}) collective-permute-start(bf16[2,256,2048]{2,1,0:T(8,128)(2,1)} %get-tuple-element.29), channel_id=1, source_target_pairs={{0,1},{1,0},{2,3},{3,2},{4,5},{5,4},{6,7},{7,6},{8,9},{9,8},{10,11... | collective-permute-start | bytes 6291464 | tf_op jit(solution)/shard_map/ppermute | solution.py:209
  544.8 108.4 %collective-permute-start.15 = (bf16[2,256,2048]{2,1,0:T(8,128)(2,1)}, bf16[2,256,2048]{2,1,0:T(8,128)(2,1)S(1)}, u32[]{:S(2)}, u32[]{:S(2)}) collective-permute-start(bf16[2,256,2048]{2,1,0:T(8,128)(2,1)} %get-tuple-element.30), channel_id=1, source_target_pairs={{0,3},{1,2},{4,7},{5,6},{8,11},{9,10},{12,15},{13,14},{16,19},{17,... | collective-permute-start | bytes 6291464 | tf_op jit(solution)/shard_map/ppermute | solution.py:209
  547.2 106.0 %collective-permute-start.16 = (bf16[2,256,2048]{2,1,0:T(8,128)(2,1)}, bf16[2,256,2048]{2,1,0:T(8,128)(2,1)}, u32[]{:S(2)}, u32[]{:S(2)}) collective-permute-start(bf16[2,256,2048]{2,1,0:T(8,128)(2,1)} %get-tuple-element.31), channel_id=1, source_target_pairs={{0,1},{1,0},{2,3},{3,2},{4,5},{5,4},{6,7},{7,6},{8,9},{9,8},{10,11... | collective-permute-start | bytes 6291464 | tf_op jit(solution)/shard_map/ppermute | solution.py:209
  626.8 16.9 %copy-start.2 = (f32[16]{0:T(128)}, f32[16]{0:T(128)S(1)}, u32[]{:S(2)}) copy-start(f32[16]{0:T(128)S(1)} %pmax.7) | copy-start | bytes 196
  626.9 47.2 %collective-permute-start.17 = (bf16[2,256,2048]{2,1,0:T(8,128)(2,1)}, bf16[2,256,2048]{2,1,0:T(8,128)(2,1)S(1)}, u32[]{:S(2)}, u32[]{:S(2)}) collective-permute-start(bf16[2,256,2048]{2,1,0:T(8,128)(2,1)} %get-tuple-element.32), channel_id=1, source_target_pairs={{0,2},{1,3},{4,6},{5,7},{8,10},{9,11},{12,14},{13,15},{16,18},{17,... | collective-permute-start | bytes 6291464 | tf_op jit(solution)/shard_map/ppermute | solution.py:209
  653.1 20.9 %copy-start = (bf16[2,256,2048]{2,1,0:T(8,128)(2,1)S(1)}, bf16[2,256,2048]{2,1,0:T(8,128)(2,1)}, u32[]{:S(2)}) copy-start(bf16[2,256,2048]{2,1,0:T(8,128)(2,1)} %get-tuple-element.33) | copy-start | bytes 6291460

commit v2 on v0

v2 whole, which is shorter than its diff:
```python
import functools

import jax
import jax.numpy as jnp
from jax import lax
from jax.experimental import pallas as pl
from jax.experimental.pallas import tpu as pltpu
from jax.sharding import PartitionSpec as P


HEAD_DIM = 128
TAU_CLIP = 100.0
ROPE_THETA = 50000.0
GROUP = 2 * HEAD_DIM
MOVED_ROWS = 2
NEG = -1e30


def rope_tables(pos_ids):
    half_dim = HEAD_DIM // 2
    inv_freq = jnp.float32(ROPE_THETA) ** (-jnp.arange(half_dim, dtype=jnp.float32) * (2.0 / HEAD_DIM))
    angle = pos_ids.astype(jnp.float32)[:, None] * inv_freq[None, :]
    cos_t, sin_t = jnp.cos(angle), jnp.sin(angle)
    return jnp.concatenate([cos_t, cos_t], axis=-1), jnp.concatenate([-sin_t, sin_t], axis=-1)


def rows_kernel(mode, first_row, meta, hidden, sib, *refs):
    remote = () if mode == "near" else refs[:2]
    w_q, w_k, w_v, w_o, cos_t, sin_t = refs[len(remote):len(remote) + 6]
    n_dst = 4 if mode == "whole" else 2
    out_refs = refs[len(refs) - 5 - n_dst - 1:len(refs) - 5]
    dsts, top = out_refs[:n_dst], out_refs[n_dst]
    x_scr, att, o_scr, wo_scr, sems = refs[len(refs) - 5:]
    row, step = pl.program_id(0), pl.program_id(1)
    n_rows, n_steps = pl.num_programs(0), pl.num_programs(1)
    chip, core = meta[0], meta[1]
    piece = hidden.shape[1]
    half = hidden.shape[0] // 2
    scale = HEAD_DIM ** -0.5
    active = 1 if mode == "far" else 0
    local_at, remote_at = (2, 0) if mode == "far" else (0, 2)

    def load(r, go):
        buf = r % 2

        def one(src, slot, sem):
            at = pl.multiple_of(slot * piece, piece)
            cp = pltpu.make_async_copy(src, x_scr.at[buf, pl.ds(at, piece)], sems.at[buf, sem])
            cp.start() if go else cp.wait()

        one(hidden.at[core * half + first_row + r], local_at + core, 0)
        one(sib.at[first_row + r], local_at + 1 - core, 1)
        if remote:
            one(remote[0].at[r], remote_at + core, 2)
            one(remote[1].at[r], remote_at + 1 - core, 3)

    def store(r, go):
        slots = (core, 1 - core, 2 + core, 3 - core)[:n_dst]
        for n, (dst, slot) in enumerate(zip(dsts, slots)):
            at = pl.multiple_of(slot * piece, piece)
            if mode == "whole":
                to = dst.at[r]
            else:
                to = dst.at[core * half + first_row + r] if n == 0 else dst.at[first_row + r]
            cp = pltpu.make_async_copy(o_scr.at[pl.ds(at, piece)], to, sems.at[2, n])
            cp.start() if go else cp.wait()

    def wo_copy():
        return pltpu.make_async_copy(w_o, wo_scr, sems.at[3, 0])

    def dot(a, b):
        return jnp.dot(a, b, preferred_element_type=jnp.float32)

    def rotated(t, base):
        pos = pl.ds(pl.multiple_of(base * piece, piece), t.shape[0])
        cos_p, sin_p = cos_t[pos, :], sin_t[pos, :]
        parts = []
        for h in range(2):
            th = t[:, h * HEAD_DIM:(h + 1) * HEAD_DIM]
            parts.append((th * cos_p + pltpu.roll(th, HEAD_DIM // 2, axis=1) * sin_p).astype(jnp.bfloat16))
        return parts

    def group():
        buf = row % 2
        x_q_at = 2 * piece if mode == "far" else 0
        n_q = 4 if mode == "whole" else 2
        x_q = x_scr[buf, x_q_at:x_q_at + n_q * piece, :]
        q_base = 2 if mode == "far" else 0
        q = rotated(dot(x_q, w_q[...]), q_base)
        k_own = rotated(dot(x_q, w_k[...]), q_base)
        if mode == "far":
            x_far = x_scr[buf, :2 * piece, :]
            k_far = rotated(dot(x_far, w_k[...]), 0)
        causal = lax.broadcasted_iota(jnp.int32, (piece, piece), 0) >= lax.broadcasted_iota(jnp.int32, (piece, piece), 1)
        nt = (((1,), (1,)), ((), ()))

        def logits(a, b):
            return lax.dot_general(a, b, nt, preferred_element_type=jnp.float32)

        scores = []
        for h in range(2):
            groups = []
            if mode == "far":
                groups.append((0, logits(q[h], k_far[h])))
            for j in range(n_q):
                groups.append((j, logits(q[h][j * piece:], k_own[h][j * piece:(j + 1) * piece])))
            scores.append(groups)
        v_own = dot(x_q, w_v[...]).astype(jnp.bfloat16)
        if mode == "far":
            v_far = dot(x_far, w_v[...]).astype(jnp.bfloat16)
        for h in range(2):
            cols = slice(h * HEAD_DIM, (h + 1) * HEAD_DIM)
            values = [v_far[:, cols]] if mode == "far" else []
            values += [v_own[j * piece:(j + 1) * piece, cols] for j in range(n_q)]
            probs = [[] for _ in values]
            inverse, best = [], None
            for i in range(n_q):
                parts = []
                for g, (start, s) in enumerate(scores[h]):
                    if start <= i:
                        part = s[(i - start) * piece:(i - start + 1) * piece]
                        diagonal = g == len(scores[h]) - n_q + i
                        parts.append((g, jnp.where(causal, part, NEG) if diagonal else part))
                m = functools.reduce(jnp.maximum, [jnp.max(part, axis=1, keepdims=True) for _, part in parts])
                total = None
                for g, part in parts:
                    p = jnp.exp((part - m) * scale)
                    add = jnp.sum(p, axis=1, keepdims=True)
                    total = add if total is None else total + add
                    probs[g].append(p.astype(jnp.bfloat16))
                inverse.append(1.0 / total)
                m_top = jnp.max(m)
                best = m_top if best is None else jnp.maximum(best, m_top)
            weighted = [dot(jnp.concatenate(p, axis=0), v) for p, v in zip(probs, values)]
            col = pl.ds(pl.multiple_of(step * GROUP + h * HEAD_DIM, HEAD_DIM), HEAD_DIM)
            for i in range(n_q):
                acc = None
                for (start, _), w in zip(scores[h], weighted):
                    if start <= i:
                        part = w[(i - start) * piece:(i - start + 1) * piece]
                        acc = part if acc is None else acc + part
                att[i * piece:(i + 1) * piece, col] = (acc * inverse[i]).astype(jnp.bfloat16)
            top[0, 0, h, :] = jnp.full((top.shape[3],), best * scale, jnp.float32)

    top[...] = jnp.full(top.shape, -jnp.inf, jnp.float32)

    @pl.when(chip == active)
    def _():
        @pl.when(step == 0)
        def _():
            @pl.when(row == 0)
            def _():
                load(0, True)
                wo_copy().start()

            load(row, False)

            @pl.when(row + 1 < n_rows)
            def _():
                load(row + 1, True)

        group()

        @pl.when(step == n_steps - 1)
        def _():
            @pl.when(row == 0)
            def _():
                wo_copy().wait()

            width = wo_scr.shape[1]
            cut = min(512, width)
            for n in range(0, width, cut):
                o_scr[:, n:n + cut] = dot(att[...], wo_scr[:, n:n + cut]).astype(jnp.bfloat16)
            store(row, True)
            store(row, False)


def rows_call(mode, first_row, n_rows, chain, meta, hidden, sib, remote, weights, tables):
    piece, d_model = hidden.shape[1:]
    w_q, w_k, w_v, w_o = weights
    width = w_q.shape[1]
    n_steps = width // GROUP
    active = 1 if mode == "far" else 0
    any_spec = pl.BlockSpec(memory_space=pl.ANY)
    w_spec = pl.BlockSpec((d_model, GROUP), lambda r, g, m: (0, jnp.where(m[0] == active, g, 0)))
    t_spec = pl.BlockSpec(tables[0].shape, lambda r, g, m: (0, 0), pipeline_mode=pl.Buffered(1))
    n_q = 4 if mode == "whole" else 2
    x_len = (2 if mode == "near" else 4) * piece
    if mode == "whole":
        out_shape = [jax.ShapeDtypeStruct((n_rows, piece, d_model), jnp.bfloat16)] * 4
    else:
        out_shape = [jax.ShapeDtypeStruct(hidden.shape, jnp.bfloat16), jax.ShapeDtypeStruct(sib.shape, jnp.bfloat16)]
    n_dst = len(out_shape)
    out_shape = out_shape + [jax.ShapeDtypeStruct((n_rows, n_steps, 8, 128), jnp.float32)]
    n_in = 2 + len(remote) + 6
    blocks = {"near": 3, "far": 7, "whole": 10}[mode]
    projections = {"near": 2 * 4, "far": 2 * 6, "whole": 4 * 4}[mode]
    flops = n_rows * (2 * projections * piece * d_model * width + 8 * blocks * piece * piece * width)
    return pl.pallas_call(
        functools.partial(rows_kernel, mode, first_row),
        out_shape=out_shape,
        grid_spec=pltpu.PrefetchScalarGridSpec(
            num_scalar_prefetch=1,
            grid=(n_rows, n_steps),
            in_specs=[any_spec] * (2 + len(remote)) + [w_spec] * 3 + [any_spec, t_spec, t_spec] + [any_spec] * len(chain),
            out_specs=[any_spec] * n_dst + [pl.BlockSpec((1, 1, 8, 128), lambda r, g, m: (r, g, 0, 0))],
            scratch_shapes=[
                pltpu.VMEM((2, x_len, d_model), jnp.bfloat16),
                pltpu.VMEM((n_q * piece, width), jnp.bfloat16),
                pltpu.VMEM((n_q * piece, d_model), jnp.bfloat16),
                pltpu.VMEM((width, d_model), jnp.bfloat16),
                pltpu.SemaphoreType.DMA((4, 4)),
            ],
        ),
        compiler_params=pltpu.CompilerParams(dimension_semantics=("arbitrary", "arbitrary"), vmem_limit_bytes=66_000_000),
        cost_estimate=pl.CostEstimate(flops=flops, bytes_accessed=40_000_000 * n_rows, transcendentals=0),
        input_output_aliases={1 + n_in + n: n for n in range(len(chain))},
    )(meta, hidden, sib, *remote, w_q, w_k, w_v, w_o, *tables, *chain)


def clip_weights(head_max, w_q, w_k):
    factor = jnp.where(head_max > TAU_CLIP, jnp.sqrt(TAU_CLIP / head_max), 1.0)
    col_factor = jnp.repeat(factor, HEAD_DIM)[None, :]
    return (w_q.astype(jnp.float32) * col_factor).astype(jnp.bfloat16), (w_k.astype(jnp.float32) * col_factor).astype(jnp.bfloat16)


def solution(mesh):
    in_chip = [(0, 1), (1, 0), (2, 3), (3, 2)]
    up = [(0, 2), (1, 3)], [(0, 3), (1, 2)]
    down = [(2, 0), (3, 1)], [(2, 1), (3, 0)]

    def layer(hidden, pos_ids, w_q, w_k, w_v, w_o):
        rank = lax.axis_index("cp")
        chip, core = rank // 2, rank % 2
        meta = jnp.stack([chip, core]).astype(jnp.int32)
        half = hidden.shape[0] // 2
        kept = half - MOVED_ROWS
        weights = (w_q, w_k, w_v, w_o)

        def send(x, pairs):
            return lax.ppermute(x, "cp", pairs)

        all_pos, hidden = lax.optimization_barrier((lax.all_gather(pos_ids, "cp", tiled=True), hidden))
        tables = rope_tables(all_pos)

        def row_of(array, which, row):
            return lax.dynamic_slice_in_dim(array, which * half + row, 1, axis=0)

        mine, other = {}, {}
        later = hidden
        for rows in ([0], [kept], [r for r in range(half) if r not in (0, kept)]):
            fetched = [row_of(later, which, r) for r in rows for which in (core, 1 - core)]
            later, *fetched = lax.optimization_barrier((later, *fetched))
            for n, r in enumerate(rows):
                mine[r], other[r] = fetched[2 * n], fetched[2 * n + 1]
        sib = send(lax.dynamic_slice_in_dim(later, (1 - core) * half, half, axis=0), in_chip)
        remote = []
        for r in range(half):
            straight, cross = up if r < kept else down
            remote.append((send(mine[r], straight), send(other[r], cross)))

        def call(mode, row, n_rows, chain):
            far_in = () if mode == "near" else remote[row]
            return rows_call(mode, row, n_rows, chain, meta, hidden, sib, far_in, weights, tables)

        first = (kept + 2) // 3
        out, give, *tops = call("near", 0, first, ())
        wholes = [call("whole", r, 1, ()) for r in range(kept, half)]
        for r in range(kept):
            if r == 2:
                out, give, top = call("near", first, kept - first, (out, give))
                tops.append(top)
            out, give, top = call("far", r, 1, (out, give))
            tops.append(top)
        got = send(give, in_chip)
        out = lax.dynamic_update_slice_in_dim(out, lax.slice_in_dim(got, 0, kept, axis=0), (1 - core) * half, axis=0)
        for r, (keep, pass_on, straight, cross, top) in zip(range(kept, half), wholes):
            tops.append(top)
            pass_on = send(pass_on, in_chip)
            keep = jnp.where(chip == 1, send(straight, up[0]), keep)
            pass_on = jnp.where(chip == 1, send(cross, up[1]), pass_on)
            out = lax.dynamic_update_slice_in_dim(out, keep, core * half + r, axis=0)
            out = lax.dynamic_update_slice_in_dim(out, pass_on, (1 - core) * half + r, axis=0)
        tops = jnp.concatenate([top.max(axis=0)[None, :, :2, 0] for top in tops], axis=0)
        head_max = lax.pmax(lax.pmax(tops.max(axis=0).reshape(-1), "cp"), "dp")
        w_q_new, w_k_new = clip_weights(head_max, w_q, w_k)
        return out, head_max, w_q_new, w_k_new


    return jax.shard_map(
        layer,
        mesh=mesh,
        in_specs=(P("dp", "cp", None), P("cp"), P(None, None), P(None, None), P(None, None), P(None, None)),
        out_specs=(P("dp", "cp", None), P(None), P(None, None), P(None, None)),
        check_vma=False,
    )
```

time: 2180 us -> 668 us (0.31)
  waiting for transfers between devices: 1070 us -> 114 us
  Pallas kernels: 0 us -> 402 us
  local copies, waits for them, and re-layouts: 308 us -> 30.9 us
  matrix products: 242 us -> 0 us
  starting transfers between devices: 217 us -> 51.2 us
  other arithmetic: 187 us -> 23.8 us
  blocking collectives: 141 us -> 37 us
    ppermute x6 -> x24, waiting for transfers between devices: 1070 us -> 114 us  [send(): return lax.ppermute(x, 'cp', pairs)]
    pallas_call x0 -> x10, Pallas kernels: none -> 402 us  [rows_call(): pl.pallas_call(functools.partial(rows_kernel, mode, first_row), out_shape...]
    dot_general x6 -> x0, matrix products: 242 us -> none  [the longest x1 43.4 us: attend_block(): jnp.einsum('bhqk,bkhd->bqhd', prob_w.astype(jnp.bfloat16), v_blk, preferr...]
    ppermute x6 -> x24, starting transfers between devices: 217 us -> 51.2 us  [send(): return lax.ppermute(x, 'cp', pairs)]
    while x8 -> x0, local copies, waits for them, and re-layouts: 148 us -> none
    pmax x1 -> x2, blocking collectives: 141 us -> 30.7 us  [layer(): head_max = lax.pmax(lax.pmax(tops.max(axis=0).reshape(-1), 'cp'), 'dp')]
    another operation x2 -> x1, other arithmetic: 97.1 us -> 0.65 us  [layer(): meta = jnp.stack([chip, core]).astype(jnp.int32)]
    slice x2 -> x0, local copies, waits for them, and re-layouts: 89.4 us -> none  [rope_rotate(): lead_half = tensor[..., :half_dim]]
  transfers between devices with their start and end apart: 6 -> 24, of which waited for: 6 -> 7; matrix products, arithmetic and copies ran while one was open for 0% -> 4% of each run, Pallas kernels for 0% -> 61%
where the time goes in v2:
time: 668 us; the launch traced here: 660 us
  Pallas kernels  402 us (60%)
  waiting for transfers between devices  114 us (17%)
  starting transfers between devices  51.2 us (8%)
  blocking collectives  37 us (6%)
  local copies, waits for them, and re-layouts  30.9 us (5%)
  other arithmetic  23.8 us (4%)
    pallas_call x10, Pallas kernels, rows_call(): pl.pallas_call(functools.partial(rows_kernel, mode, first_row), out_shape...  402 us
    ppermute x24, waiting for transfers between devices, send(): return lax.ppermute(x, 'cp', pairs)  114 us
    ppermute x24, starting transfers between devices, send(): return lax.ppermute(x, 'cp', pairs)  51.2 us
    pmax x2, blocking collectives, layer(): head_max = lax.pmax(lax.pmax(tops.max(axis=0).reshape(-1), 'cp'), 'dp')  30.7 us
    dynamic_slice x3, local copies, waits for them, and re-layouts, row_of(): return lax.dynamic_slice_in_dim(array, which * half + row, 1, axis=0)  15.6 us
    convert_element_type x1, other arithmetic, clip_weights(): (w_k.astype(jnp.float32) * col_factor).astype(jnp.bfloat16)  13.4 us
  transfers between devices with their start and end apart: 24, of which 7 were waited for; matrix products, arithmetic and copies ran while one was open for 4% of the time, Pallas kernels for 61%

profile of v2, /device:TPU:0, one launch (start us, length us, event | category | flops | bytes accessed | tf_op | source)
XLA Modules:
  0.0 660.1 jit_solution(15698687385419395785)
XLA Ops:
  0.7 6.3 all-gather
  6.9 3.1 constant_dynamic-slice_fusion.15
  10.1 3.1 constant_dynamic-slice_fusion.13
  13.2 9.3 %constant_dynamic-slice_fusion.1 = (bf16[1,256,2048]{2,1,0:T(8,128)(2,1)}, bf16[1,256,2048]{2,1,0:T(8,128)(2,1)}, bf16[1,256,2048]{2,1,0:T(8,128)(2,1)}, bf16[1,...) fusion(bf16[16,256,2048]{2,1,0:T(8,128)(2,1)} %hidden.9, ...), kind=kLoop, calls=%fused_computation.23 | loop fusion | bytes 25165872 | tf_op jit(solution)/shard_map/dynamic_slice | solution.py:247
  22.5 8.4 %constant_dynamic-slice_fusion = bf16[8,256,2048]{2,1,0:T(8,128)(2,1)} fusion(bf16[16,256,2048]{2,1,0:T(8,128)(2,1)} %hidden.9, s32[]{:T(128)S(6)} %select_n.92), kind=kLoop, calls=%fused_computation.22 | loop fusion | bytes 16777220 | tf_op jit(solution)/shard_map/dynamic_slice | solution.py:256
  31.3 4.8 collective-permute-start.11
  36.2 2.3 collective-permute-start.12
  38.4 2.3 collective-permute-start.10
  40.7 2.3 collective-permute-start.9
  43.6 1.9 fusion
  46.9 2.5 collective-permute-start.7
  49.4 74.8 %shard_map.93 = (bf16[16,256,2048]{2,1,0:T(8,128)(2,1)}, bf16[8,256,2048]{2,1,0:T(8,128)(2,1)}, f32[2,8,8,128]{3,2,1,0:T(8,128)}) custom-call(s32[2]{0:T(128)} %pad_add_fusion.meta, bf16[16,256,2048]{2,1,0:T(8,128)(2,1)} %hidden.9, bf16[8,256,2048]{2,1,0:T(8,128)(2,1)} %collective-permute-done.sib, bf16[2048,2048]{1,0:T(8,128)(2,1)} %refs_2_.19, ...), custom_call_target="tpu_custom_call" | custom-call | flops 40802189312 | bytes 80000000 | tf_op jit(solution)/shard_map/pallas_call | solution.py:199
  124.2 2.3 collective-permute-start.8
  126.5 2.4 collective-permute-start.5
  128.9 5.4 shard_map.94
  134.3 7.8 %collective-permute-start.6 = (bf16[1,256,2048]{2,1,0:T(8,128)(2,1)}, bf16[1,256,2048]{2,1,0:T(8,128)(2,1)}, u32[]{:S(2)}, u32[]{:S(2)}) collective-permute-start(bf16[1,256,2048]{2,1,0:T(8,128)(2,1)} %get-tuple-element.69), channel_id=1, source_target_pairs={{0,3},{1,2},{4,7},{5,6},{8,11},{9,10},{12,15},{13,14},{16,19},{17,... | collective-permute-start | bytes 3145736 | tf_op jit(solution)/shard_map/ppermute | solution.py:241
  142.2 2.4 collective-permute-start.3
  144.6 5.4 shard_map.95
  150.0 144.2 %shard_map.96 = (bf16[16,256,2048]{2,1,0:T(8,128)(2,1)}, bf16[8,256,2048]{2,1,0:T(8,128)(2,1)}, f32[4,8,8,128]{3,2,1,0:T(8,128)}) custom-call(s32[2]{0:T(128)} %pad_add_fusion.meta, bf16[16,256,2048]{2,1,0:T(8,128)(2,1)} %hidden.9, bf16[8,256,2048]{2,1,0:T(8,128)(2,1)} %collective-permute-done.sib, ...), custom_call_target="tpu_custom_call", output_to_operand_aliasing={{0}: (9, {}), {1}: (10, {})} | custom-call | flops 81604378624 | bytes 160000000 | tf_op jit(solution)/shard_map/pallas_call | solution.py:199
  294.2 2.6 collective-permute-start.4
  296.8 2.3 collective-permute-start.1
  299.0 5.4 shard_map.97
  304.4 2.3 collective-permute-start.2
  306.7 1.7 collective-permute-start.19
  308.5 5.4 shard_map.98
  315.2 4.4 collective-permute-done.4.refs_1_
  319.6 1.5 collective-permute-start.14
  321.0 5.4 shard_map.99
  326.5 15.6 %collective-permute-done.1.refs_0_ = bf16[1,256,2048]{2,1,0:T(8,128)(2,1)} collective-permute-done((bf16[1,256,2048]{2,1,0:T(8,128)(2,1)}, bf16[1,256,2048]{2,1,0:T(8,128)(2,1)}, u32[]{:S(2)}, u32[]{:S(2)}) %collective-permute-start.1) | collective-permute-done | bytes 1048608 | tf_op jit(solution)/shard_map/ppermute | solution.py:241
  342.1 1.5 collective-permute-start.15
  343.6 19.5 %collective-permute-done.2.refs_1_ = bf16[1,256,2048]{2,1,0:T(8,128)(2,1)} collective-permute-done((bf16[1,256,2048]{2,1,0:T(8,128)(2,1)}, bf16[1,256,2048]{2,1,0:T(8,128)(2,1)}, u32[]{:S(2)}, u32[]{:S(2)}) %collective-permute-start.2) | collective-permute-done | bytes 1048608 | tf_op jit(solution)/shard_map/ppermute | solution.py:241
  363.0 5.4 shard_map.100
  368.5 19.7 %collective-permute-done.20.refs_1_ = bf16[1,256,2048]{2,1,0:T(8,128)(2,1)} collective-permute-done((bf16[1,256,2048]{2,1,0:T(8,128)(2,1)}, bf16[1,256,2048]{2,1,0:T(8,128)(2,1)}, u32[]{:S(2)}, u32[]{:S(2)}) %collective-permute-start.20) | collective-permute-done | bytes 1048608 | tf_op jit(solution)/shard_map/ppermute | solution.py:241
  388.2 75.2 %shard_map.102 = (bf16[1,256,2048]{2,1,0:T(8,128)(2,1)}, bf16[1,256,2048]{2,1,0:T(8,128)(2,1)}, bf16[1,256,2048]{2,1,0:T(8,128)(2,1)}, bf16[1,256,2048]{2,1,0:T(8,128)(2,1)}, f32[1,8,8,128]{3,2,1,0:T(8,128)}) custom-call(s32[2]{0:T(128)} %pad_add_fusion.meta, bf16[16,256,2048]{2,1,0:T(8,128)(2,1)} %hidden.9, bf16[8,256,2048]{2,1,0:T(8,128)(2,1)} %collective-permute-done.sib, ...), custom_call_target="tpu_custom_call" | custom-call | flops 45097156608 | bytes 40000000 | tf_op jit(solution)/shard_map/pallas_call | solution.py:199
  463.5 75.0 %shard_map.101 = (bf16[1,256,2048]{2,1,0:T(8,128)(2,1)}, bf16[1,256,2048]{2,1,0:T(8,128)(2,1)}, bf16[1,256,2048]{2,1,0:T(8,128)(2,1)}, bf16[1,256,2048]{2,1,0:T(8,128)(2,1)}, f32[1,8,8,128]{3,2,1,0:T(8,128)}) custom-call(s32[2]{0:T(128)} %pad_add_fusion.meta, bf16[16,256,2048]{2,1,0:T(8,128)(2,1)} %hidden.9, bf16[8,256,2048]{2,1,0:T(8,128)(2,1)} %collective-permute-done.sib, ...), custom_call_target="tpu_custom_call" | custom-call | flops 45097156608 | bytes 40000000 | tf_op jit(solution)/shard_map/pallas_call | solution.py:199
  539.6 9.0 %pmax.14 = f32[16]{0:T(128)S(1)} all-reduce(f32[16]{0:T(128)S(1)} %reshape.63), channel_id=1, replica_groups=mesh['dp'=8,'cp'=4] {'cp'}, use_global_device_ids=true, to_apply=%region_2.3 | all-reduce | flops 16 | bytes 128 | tf_op jit(solution)/shard_map/pmax | solution.py:285
  548.6 21.7 %pmax.15 = f32[16]{0:T(128)S(1)} all-reduce(f32[16]{0:T(128)S(1)} %pmax.14), channel_id=1, replica_groups=mesh['dp'=8,'cp'=4] {'dp'}, use_global_device_ids=true, to_apply=%region_3.4 | all-reduce | flops 16 | bytes 128 | tf_op jit(solution)/shard_map/pmax | solution.py:285
  570.3 3.6 collective-permute-start.16
  574.0 13.4 %multiply_convert_fusion = (bf16[2048,2048]{1,0:T(8,128)(2,1)}, bf16[2048,2048]{1,0:T(8,128)(2,1)}) fusion(bf16[2048,2048]{1,0:T(8,128)(2,1)} %refs_3_.19, f32[2048]{0:T(1024)S(1)} %broadcast_bitcast_fusion, bf16[2048,2048]{1,0:T(8,128)(2,1)} %refs_2_.19), kind=kLoop, calls=%fused_computation | loop fusion | flops 25165824 | bytes 33562624 | tf_op jit(solution)/shard_map/convert_element_type | solution.py:224
  587.4 1.7 collective-permute-start.17
  592.0 6.6 %slice_dynamic-update-slice_fusion = bf16[16,256,2048]{2,1,0:T(8,128)(2,1)} fusion(bf16[16,256,2048]{2,1,0:T(8,128)(2,1)} %get-tuple-element.90, s32[]{:T(128)S(6)} %select_n.92, bf16[8,256,2048]{2,1,0:T(8,128)(2,1)} %collective-permute-done.13), kind=kLoop, calls=%fused_computation.2 | loop fusion | bytes 12582916 | tf_op jit(solution)/shard_map/dynamic_update_slice | solution.py:276
  599.1 1.4 select_dynamic-update-slice_fusion.3
  600.5 14.8 %collective-permute-done.17 = bf16[1,256,2048]{2,1,0:T(8,128)(2,1)S(1)} collective-permute-done((bf16[1,256,2048]{2,1,0:T(8,128)(2,1)S(1)}, bf16[1,256,2048]{2,1,0:T(8,128)(2,1)S(1)}, u32[]{:S(2)}, u32[]{:S(2)}) %collective-permute-start.17) | collective-permute-done | bytes 1048608 | tf_op jit(solution)/shard_map/ppermute | solution.py:241
  615.3 1.4 select_dynamic-update-slice_fusion.2
  616.6 21.1 %collective-permute-done.21 = bf16[1,256,2048]{2,1,0:T(8,128)(2,1)S(1)} collective-permute-done((bf16[1,256,2048]{2,1,0:T(8,128)(2,1)S(1)}, bf16[1,256,2048]{2,1,0:T(8,128)(2,1)S(1)}, u32[]{:S(2)}, u32[]{:S(2)}) %collective-permute-start.21) | collective-permute-done | bytes 1048608 | tf_op jit(solution)/shard_map/ppermute | solution.py:241
  637.7 1.4 select_dynamic-update-slice_fusion.1
  639.1 19.4 %collective-permute-done.22 = bf16[1,256,2048]{2,1,0:T(8,128)(2,1)S(1)} collective-permute-done((bf16[1,256,2048]{2,1,0:T(8,128)(2,1)S(1)}, bf16[1,256,2048]{2,1,0:T(8,128)(2,1)S(1)}, u32[]{:S(2)}, u32[]{:S(2)}) %collective-permute-start.22) | collective-permute-done | bytes 1048608 | tf_op jit(solution)/shard_map/ppermute | solution.py:241
  658.5 1.4 select_dynamic-update-slice_fusion
  (54 shorter events, 8.2 us)
Async XLA Ops:
  31.0 15.9 %collective-permute-start = (bf16[8,256,2048]{2,1,0:T(8,128)(2,1)}, bf16[8,256,2048]{2,1,0:T(8,128)(2,1)}, u32[]{:S(2)}, u32[]{:S(2)}) collective-permute-start(bf16[8,256,2048]{2,1,0:T(8,128)(2,1)} %constant_dynamic-slice_fusion), channel_id=1, source_target_pairs={{0,1},{1,0},{2,3},{3,2},{4,5},{5,4},{6,7},{7,6},{8,9},{9,8},{10,11... | collective-permute-start | bytes 25165832 | tf_op jit(solution)/shard_map/ppermute | solution.py:241
  31.3 92.8 %collective-permute-start.11 = (bf16[1,256,2048]{2,1,0:T(8,128)(2,1)}, bf16[1,256,2048]{2,1,0:T(8,128)(2,1)}, u32[]{:S(2)}, u32[]{:S(2)}) collective-permute-start(bf16[1,256,2048]{2,1,0:T(8,128)(2,1)} %get-tuple-element.74), channel_id=1, source_target_pairs={{0,2},{1,3},{4,6},{5,7},{8,10},{9,11},{12,14},{13,15},{16,18},{17,... | collective-permute-start | bytes 3145736 | tf_op jit(solution)/shard_map/ppermute | solution.py:241
  36.2 90.3 %collective-permute-start.12 = (bf16[1,256,2048]{2,1,0:T(8,128)(2,1)}, bf16[1,256,2048]{2,1,0:T(8,128)(2,1)}, u32[]{:S(2)}, u32[]{:S(2)}) collective-permute-start(bf16[1,256,2048]{2,1,0:T(8,128)(2,1)} %get-tuple-element.75), channel_id=1, source_target_pairs={{0,3},{1,2},{4,7},{5,6},{8,11},{9,10},{12,15},{13,14},{16,19},{17,... | collective-permute-start | bytes 3145736 | tf_op jit(solution)/shard_map/ppermute | solution.py:241
  38.4 95.9 %collective-permute-start.10 = (bf16[1,256,2048]{2,1,0:T(8,128)(2,1)}, bf16[1,256,2048]{2,1,0:T(8,128)(2,1)}, u32[]{:S(2)}, u32[]{:S(2)}) collective-permute-start(bf16[1,256,2048]{2,1,0:T(8,128)(2,1)} %get-tuple-element.73), channel_id=1, source_target_pairs={{0,3},{1,2},{4,7},{5,6},{8,11},{9,10},{12,15},{13,14},{16,19},{17,... | collective-permute-start | bytes 3145736 | tf_op jit(solution)/shard_map/ppermute | solution.py:241
  40.7 101.5 %collective-permute-start.9 = (bf16[1,256,2048]{2,1,0:T(8,128)(2,1)}, bf16[1,256,2048]{2,1,0:T(8,128)(2,1)}, u32[]{:S(2)}, u32[]{:S(2)}) collective-permute-start(bf16[1,256,2048]{2,1,0:T(8,128)(2,1)} %get-tuple-element.72), channel_id=1, source_target_pairs={{0,2},{1,3},{4,6},{5,7},{8,10},{9,11},{12,14},{13,15},{16,18},{17,... | collective-permute-start | bytes 3145736 | tf_op jit(solution)/shard_map/ppermute | solution.py:241
  46.9 247.3 %collective-permute-start.7 = (bf16[1,256,2048]{2,1,0:T(8,128)(2,1)}, bf16[1,256,2048]{2,1,0:T(8,128)(2,1)}, u32[]{:S(2)}, u32[]{:S(2)}) collective-permute-start(bf16[1,256,2048]{2,1,0:T(8,128)(2,1)} %get-tuple-element.70), channel_id=1, source_target_pairs={{0,2},{1,3},{4,6},{5,7},{8,10},{9,11},{12,14},{13,15},{16,18},{17,... | collective-permute-start | bytes 3145736 | tf_op jit(solution)/shard_map/ppermute | solution.py:241
  124.2 172.6 %collective-permute-start.8 = (bf16[1,256,2048]{2,1,0:T(8,128)(2,1)}, bf16[1,256,2048]{2,1,0:T(8,128)(2,1)}, u32[]{:S(2)}, u32[]{:S(2)}) collective-permute-start(bf16[1,256,2048]{2,1,0:T(8,128)(2,1)} %get-tuple-element.71), channel_id=1, source_target_pairs={{0,3},{1,2},{4,7},{5,6},{8,11},{9,10},{12,15},{13,14},{16,19},{17,... | collective-permute-start | bytes 3145736 | tf_op jit(solution)/shard_map/ppermute | solution.py:241
  126.5 178.0 %collective-permute-start.5 = (bf16[1,256,2048]{2,1,0:T(8,128)(2,1)}, bf16[1,256,2048]{2,1,0:T(8,128)(2,1)}, u32[]{:S(2)}, u32[]{:S(2)}) collective-permute-start(bf16[1,256,2048]{2,1,0:T(8,128)(2,1)} %get-tuple-element.68), channel_id=1, source_target_pairs={{0,2},{1,3},{4,6},{5,7},{8,10},{9,11},{12,14},{13,15},{16,18},{17,... | collective-permute-start | bytes 3145736 | tf_op jit(solution)/shard_map/ppermute | solution.py:241
  134.3 172.4 %collective-permute-start.6 = (bf16[1,256,2048]{2,1,0:T(8,128)(2,1)}, bf16[1,256,2048]{2,1,0:T(8,128)(2,1)}, u32[]{:S(2)}, u32[]{:S(2)}) collective-permute-start(bf16[1,256,2048]{2,1,0:T(8,128)(2,1)} %get-tuple-element.69), channel_id=1, source_target_pairs={{0,3},{1,2},{4,7},{5,6},{8,11},{9,10},{12,15},{13,14},{16,19},{17,... | collective-permute-start | bytes 3145736 | tf_op jit(solution)/shard_map/ppermute | solution.py:241
  142.2 171.8 %collective-permute-start.3 = (bf16[1,256,2048]{2,1,0:T(8,128)(2,1)}, bf16[1,256,2048]{2,1,0:T(8,128)(2,1)}, u32[]{:S(2)}, u32[]{:S(2)}) collective-permute-start(bf16[1,256,2048]{2,1,0:T(8,128)(2,1)} %get-tuple-element.66), channel_id=1, source_target_pairs={{0,2},{1,3},{4,6},{5,7},{8,10},{9,11},{12,14},{13,15},{16,18},{17,... | collective-permute-start | bytes 3145736 | tf_op jit(solution)/shard_map/ppermute | solution.py:241
  294.2 25.4 %collective-permute-start.4 = (bf16[1,256,2048]{2,1,0:T(8,128)(2,1)}, bf16[1,256,2048]{2,1,0:T(8,128)(2,1)}, u32[]{:S(2)}, u32[]{:S(2)}) collective-permute-start(bf16[1,256,2048]{2,1,0:T(8,128)(2,1)} %get-tuple-element.67), channel_id=1, source_target_pairs={{0,3},{1,2},{4,7},{5,6},{8,11},{9,10},{12,15},{13,14},{16,19},{17,... | collective-permute-start | bytes 3145736 | tf_op jit(solution)/shard_map/ppermute | solution.py:241
  296.8 45.3 %collective-permute-start.1 = (bf16[1,256,2048]{2,1,0:T(8,128)(2,1)}, bf16[1,256,2048]{2,1,0:T(8,128)(2,1)}, u32[]{:S(2)}, u32[]{:S(2)}) collective-permute-start(bf16[1,256,2048]{2,1,0:T(8,128)(2,1)} %get-tuple-element.63), channel_id=1, source_target_pairs={{0,2},{1,3},{4,6},{5,7},{8,10},{9,11},{12,14},{13,15},{16,18},{17,... | collective-permute-start | bytes 3145736 | tf_op jit(solution)/shard_map/ppermute | solution.py:241
  304.4 58.6 %collective-permute-start.2 = (bf16[1,256,2048]{2,1,0:T(8,128)(2,1)}, bf16[1,256,2048]{2,1,0:T(8,128)(2,1)}, u32[]{:S(2)}, u32[]{:S(2)}) collective-permute-start(bf16[1,256,2048]{2,1,0:T(8,128)(2,1)} %get-tuple-element.64), channel_id=1, source_target_pairs={{0,3},{1,2},{4,7},{5,6},{8,11},{9,10},{12,15},{13,14},{16,19},{17,... | collective-permute-start | bytes 3145736 | tf_op jit(solution)/shard_map/ppermute | solution.py:241
  306.7 61.8 %collective-permute-start.19 = (bf16[1,256,2048]{2,1,0:T(8,128)(2,1)}, bf16[1,256,2048]{2,1,0:T(8,128)(2,1)}, u32[]{:S(2)}, u32[]{:S(2)}) collective-permute-start(bf16[1,256,2048]{2,1,0:T(8,128)(2,1)} %get-tuple-element.98), channel_id=1, source_target_pairs={{2,0},{3,1},{6,4},{7,5},{10,8},{11,9},{14,12},{15,13},{18,16},{19,... | collective-permute-start | bytes 3145736 | tf_op jit(solution)/shard_map/ppermute | solution.py:241
  313.9 74.3 %collective-permute-start.20 = (bf16[1,256,2048]{2,1,0:T(8,128)(2,1)}, bf16[1,256,2048]{2,1,0:T(8,128)(2,1)}, u32[]{:S(2)}, u32[]{:S(2)}) collective-permute-start(bf16[1,256,2048]{2,1,0:T(8,128)(2,1)} %get-tuple-element.99), channel_id=1, source_target_pairs={{2,1},{3,0},{6,5},{7,4},{10,9},{11,8},{14,13},{15,12},{18,17},{19,... | collective-permute-start | bytes 3145736 | tf_op jit(solution)/shard_map/ppermute | solution.py:241
  319.6 143.9 %collective-permute-start.14 = (bf16[1,256,2048]{2,1,0:T(8,128)(2,1)}, bf16[1,256,2048]{2,1,0:T(8,128)(2,1)}, u32[]{:S(2)}, u32[]{:S(2)}) collective-permute-start(bf16[1,256,2048]{2,1,0:T(8,128)(2,1)} %get-tuple-element.92), channel_id=1, source_target_pairs={{2,0},{3,1},{6,4},{7,5},{10,8},{11,9},{14,12},{15,13},{18,16},{19,... | collective-permute-start | bytes 3145736 | tf_op jit(solution)/shard_map/ppermute | solution.py:241
  342.1 121.5 %collective-permute-start.15 = (bf16[1,256,2048]{2,1,0:T(8,128)(2,1)}, bf16[1,256,2048]{2,1,0:T(8,128)(2,1)}, u32[]{:S(2)}, u32[]{:S(2)}) collective-permute-start(bf16[1,256,2048]{2,1,0:T(8,128)(2,1)} %get-tuple-element.93), channel_id=1, source_target_pairs={{2,1},{3,0},{6,5},{7,4},{10,9},{11,8},{14,13},{15,12},{18,17},{19,... | collective-permute-start | bytes 3145736 | tf_op jit(solution)/shard_map/ppermute | solution.py:241
  368.4 95.0 %copy-start.2 = (f32[4,8,8,128]{3,2,1,0:T(8,128)S(1)}, f32[4,8,8,128]{3,2,1,0:T(8,128)}, u32[]{:S(2)}) copy-start(f32[4,8,8,128]{3,2,1,0:T(8,128)} %get-tuple-element.107) | copy-start | bytes 393220
  368.4 95.0 %copy-start.3 = (f32[2,8,8,128]{3,2,1,0:T(8,128)S(1)}, f32[2,8,8,128]{3,2,1,0:T(8,128)}, u32[]{:S(2)}) copy-start(f32[2,8,8,128]{3,2,1,0:T(8,128)} %get-tuple-element.104) | copy-start | bytes 196612
  368.4 222.2 %collective-permute-start.13 = (bf16[8,256,2048]{2,1,0:T(8,128)(2,1)}, bf16[8,256,2048]{2,1,0:T(8,128)(2,1)}, u32[]{:S(2)}, u32[]{:S(2)}) collective-permute-start(bf16[8,256,2048]{2,1,0:T(8,128)(2,1)} %get-tuple-element.91), channel_id=1, source_target_pairs={{0,1},{1,0},{2,3},{3,2},{4,5},{5,4},{6,7},{7,6},{8,9},{9,8},{10,11... | collective-permute-start | bytes 25165832 | tf_op jit(solution)/shard_map/ppermute | solution.py:241
  570.3 17.2 %copy-start.9 = (f32[16]{0:T(128)}, f32[16]{0:T(128)S(1)}, u32[]{:S(2)}) copy-start(f32[16]{0:T(128)S(1)} %pmax.15) | copy-start | bytes 196
  570.3 28.4 %collective-permute-start.16 = (bf16[1,256,2048]{2,1,0:T(8,128)(2,1)}, bf16[1,256,2048]{2,1,0:T(8,128)(2,1)S(1)}, u32[]{:S(2)}, u32[]{:S(2)}) collective-permute-start(bf16[1,256,2048]{2,1,0:T(8,128)(2,1)} %get-tuple-element.94), channel_id=1, source_target_pairs={{0,2},{1,3},{4,6},{5,7},{8,10},{9,11},{12,14},{13,15},{16,18},{17,... | collective-permute-start | bytes 3145736 | tf_op jit(solution)/shard_map/ppermute | solution.py:241
  573.9 13.5 %copy-start.8 = (bf16[1,256,2048]{2,1,0:T(8,128)(2,1)S(1)}, bf16[1,256,2048]{2,1,0:T(8,128)(2,1)}, u32[]{:S(2)}) copy-start(bf16[1,256,2048]{2,1,0:T(8,128)(2,1)} %get-tuple-element.96) | copy-start | bytes 3145732
  573.9 15.2 %copy-start.7 = (bf16[1,256,2048]{2,1,0:T(8,128)(2,1)S(1)}, bf16[1,256,2048]{2,1,0:T(8,128)(2,1)}, u32[]{:S(2)}) copy-start(bf16[1,256,2048]{2,1,0:T(8,128)(2,1)} %get-tuple-element.97) | copy-start | bytes 3145732
  573.9 15.3 %copy-start.6 = (bf16[1,256,2048]{2,1,0:T(8,128)(2,1)S(1)}, bf16[1,256,2048]{2,1,0:T(8,128)(2,1)}, u32[]{:S(2)}) copy-start(bf16[1,256,2048]{2,1,0:T(8,128)(2,1)} %get-tuple-element.100) | copy-start | bytes 3145732
  573.9 16.7 %copy-start.5 = (bf16[1,256,2048]{2,1,0:T(8,128)(2,1)S(1)}, bf16[1,256,2048]{2,1,0:T(8,128)(2,1)}, u32[]{:S(2)}) copy-start(bf16[1,256,2048]{2,1,0:T(8,128)(2,1)} %get-tuple-element.102) | copy-start | bytes 3145732
  574.0 24.7 %copy-start.4 = (bf16[1,256,2048]{2,1,0:T(8,128)(2,1)S(1)}, bf16[1,256,2048]{2,1,0:T(8,128)(2,1)}, u32[]{:S(2)}) copy-start(bf16[1,256,2048]{2,1,0:T(8,128)(2,1)} %get-tuple-element.103) | copy-start | bytes 3145732
  574.0 25.1 %copy-start.1 = (bf16[1,256,2048]{2,1,0:T(8,128)(2,1)S(1)}, bf16[1,256,2048]{2,1,0:T(8,128)(2,1)}, u32[]{:S(2)}) copy-start(bf16[1,256,2048]{2,1,0:T(8,128)(2,1)} %get-tuple-element.95) | copy-start | bytes 3145732
  587.4 50.3 %copy-start = (bf16[1,256,2048]{2,1,0:T(8,128)(2,1)S(1)}, bf16[1,256,2048]{2,1,0:T(8,128)(2,1)}, u32[]{:S(2)}) copy-start(bf16[1,256,2048]{2,1,0:T(8,128)(2,1)} %get-tuple-element.101) | copy-start | bytes 3145732
  587.4 27.8 %collective-permute-start.17 = (bf16[1,256,2048]{2,1,0:T(8,128)(2,1)S(1)}, bf16[1,256,2048]{2,1,0:T(8,128)(2,1)S(1)}, u32[]{:S(2)}, u32[]{:S(2)}) collective-permute-start(bf16[1,256,2048]{2,1,0:T(8,128)(2,1)S(1)} %copy-done.8), channel_id=1, source_target_pairs={{0,3},{1,2},{4,7},{5,6},{8,11},{9,10},{12,15},{13,14},{16,19},{17,... | collective-permute-start | bytes 3145736 | tf_op jit(solution)/shard_map/ppermute | solution.py:241
  589.2 26.1 %collective-permute-start.18 = (bf16[1,256,2048]{2,1,0:T(8,128)(2,1)S(1)}, bf16[1,256,2048]{2,1,0:T(8,128)(2,1)S(1)}, u32[]{:S(2)}, u32[]{:S(2)}) collective-permute-start(bf16[1,256,2048]{2,1,0:T(8,128)(2,1)S(1)} %copy-done.7), channel_id=1, source_target_pairs={{0,1},{1,0},{2,3},{3,2},{4,5},{5,4},{6,7},{7,6},{8,9},{9,8},{10,11... | collective-permute-start | bytes 3145736 | tf_op jit(solution)/shard_map/ppermute | solution.py:241
  589.3 48.4 %collective-permute-start.21 = (bf16[1,256,2048]{2,1,0:T(8,128)(2,1)S(1)}, bf16[1,256,2048]{2,1,0:T(8,128)(2,1)S(1)}, u32[]{:S(2)}, u32[]{:S(2)}) collective-permute-start(bf16[1,256,2048]{2,1,0:T(8,128)(2,1)S(1)} %copy-done.6), channel_id=1, source_target_pairs={{0,2},{1,3},{4,6},{5,7},{8,10},{9,11},{12,14},{13,15},{16,18},{17,... | collective-permute-start | bytes 3145736 | tf_op jit(solution)/shard_map/ppermute | solution.py:241
  590.7 67.8 %collective-permute-start.22 = (bf16[1,256,2048]{2,1,0:T(8,128)(2,1)S(1)}, bf16[1,256,2048]{2,1,0:T(8,128)(2,1)S(1)}, u32[]{:S(2)}, u32[]{:S(2)}) collective-permute-start(bf16[1,256,2048]{2,1,0:T(8,128)(2,1)S(1)} %copy-done.5), channel_id=1, source_target_pairs={{0,3},{1,2},{4,7},{5,6},{8,11},{9,10},{12,15},{13,14},{16,19},{17,... | collective-permute-start | bytes 3145736 | tf_op jit(solution)/shard_map/ppermute | solution.py:241
  598.6 59.8 %collective-permute-start.23 = (bf16[1,256,2048]{2,1,0:T(8,128)(2,1)S(1)}, bf16[1,256,2048]{2,1,0:T(8,128)(2,1)S(1)}, u32[]{:S(2)}, u32[]{:S(2)}) collective-permute-start(bf16[1,256,2048]{2,1,0:T(8,128)(2,1)S(1)} %copy-done.4), channel_id=1, source_target_pairs={{0,1},{1,0},{2,3},{3,2},{4,5},{5,4},{6,7},{7,6},{8,9},{9,8},{10,11... | collective-permute-start | bytes 3145736 | tf_op jit(solution)/shard_map/ppermute | solution.py:241

commit v3 on v2

--- a/solution.py
+++ b/solution.py
@@ -14,6 +14,8 @@
 GROUP = 2 * HEAD_DIM
 MOVED_ROWS = 2
 NEG = -1e30
+PACK = {"near": 2, "far": 1, "whole": 1}
+CHUNK = 32
 
 
 def rope_tables(pos_ids):
@@ -38,6 +40,9 @@
     half = hidden.shape[0] // 2
     scale = HEAD_DIM ** -0.5
     active = 1 if mode == "far" else 0
+    pack = PACK[mode]
+    n_q = 4 if mode == "whole" else 2
+    span = n_q * piece
     local_at, remote_at = (2, 0) if mode == "far" else (0, 2)
 
     def load(r, go):
@@ -48,22 +53,26 @@
             cp = pltpu.make_async_copy(src, x_scr.at[buf, pl.ds(at, piece)], sems.at[buf, sem])
             cp.start() if go else cp.wait()
 
-        one(hidden.at[core * half + first_row + r], local_at + core, 0)
-        one(sib.at[first_row + r], local_at + 1 - core, 1)
+        for b in range(pack):
+            n = first_row + r * pack + b
+            one(hidden.at[core * half + n], local_at + core + 2 * b, 2 * b)
+            one(sib.at[n], local_at + 1 - core + 2 * b, 2 * b + 1)
         if remote:
             one(remote[0].at[r], remote_at + core, 2)
             one(remote[1].at[r], remote_at + 1 - core, 3)
 
     def store(r, go):
         slots = (core, 1 - core, 2 + core, 3 - core)[:n_dst]
-        for n, (dst, slot) in enumerate(zip(dsts, slots)):
-            at = pl.multiple_of(slot * piece, piece)
-            if mode == "whole":
-                to = dst.at[r]
-            else:
-                to = dst.at[core * half + first_row + r] if n == 0 else dst.at[first_row + r]
-            cp = pltpu.make_async_copy(o_scr.at[pl.ds(at, piece)], to, sems.at[2, n])
-            cp.start() if go else cp.wait()
+        for b in range(pack):
+            for n, (dst, slot) in enumerate(zip(dsts, slots)):
+                at = pl.multiple_of(slot * piece + b * span, piece)
+                if mode == "whole":
+                    to = dst.at[r]
+                else:
+                    at_row = first_row + r * pack + b
+                    to = dst.at[core * half + at_row] if n == 0 else dst.at[at_row]
+                cp = pltpu.make_async_copy(o_scr.at[pl.ds(at, piece)], to, sems.at[2, 2 * b + n])
+                cp.start() if go else cp.wait()
 
     def wo_copy():
         return pltpu.make_async_copy(w_o, wo_scr, sems.at[3, 0])
@@ -72,55 +81,61 @@
         return jnp.dot(a, b, preferred_element_type=jnp.float32)
 
     def rotated(t, base):
-        pos = pl.ds(pl.multiple_of(base * piece, piece), t.shape[0])
-        cos_p, sin_p = cos_t[pos, :], sin_t[pos, :]
-        parts = []
-        for h in range(2):
-            th = t[:, h * HEAD_DIM:(h + 1) * HEAD_DIM]
-            parts.append((th * cos_p + pltpu.roll(th, HEAD_DIM // 2, axis=1) * sin_p).astype(jnp.bfloat16))
-        return parts
+        start = pl.multiple_of(base * piece, piece)
+        parts = [[], []]
+        for at in range(0, t.shape[0], CHUNK):
+            pos = pl.ds(start + at % (n_q * piece), CHUNK)
+            cos_p, sin_p = cos_t[pos, :], sin_t[pos, :]
+            for h in range(2):
+                th = t[at:at + CHUNK, h * HEAD_DIM:(h + 1) * HEAD_DIM]
+                parts[h].append((th * cos_p + pltpu.roll(th, HEAD_DIM // 2, axis=1) * sin_p).astype(jnp.bfloat16))
+        return [jnp.concatenate(p, axis=0) for p in parts]
 
     def group():
         buf = row % 2
         x_q_at = 2 * piece if mode == "far" else 0
-        n_q = 4 if mode == "whole" else 2
-        x_q = x_scr[buf, x_q_at:x_q_at + n_q * piece, :]
+        x_q = x_scr[buf, x_q_at:x_q_at + pack * span, :]
         q_base = 2 if mode == "far" else 0
         q = rotated(dot(x_q, w_q[...]), q_base)
         k_own = rotated(dot(x_q, w_k[...]), q_base)
         if mode == "far":
             x_far = x_scr[buf, :2 * piece, :]
             k_far = rotated(dot(x_far, w_k[...]), 0)
-        causal = lax.broadcasted_iota(jnp.int32, (piece, piece), 0) >= lax.broadcasted_iota(jnp.int32, (piece, piece), 1)
         nt = (((1,), (1,)), ((), ()))
 
         def logits(a, b):
             return lax.dot_general(a, b, nt, preferred_element_type=jnp.float32)
 
+        units = [(b, h) for b in range(pack) for h in range(2)]
         scores = []
-        for h in range(2):
+        for b, h in units:
             groups = []
+            q_b, k_b = q[h][b * span:(b + 1) * span], k_own[h][b * span:(b + 1) * span]
             if mode == "far":
-                groups.append((0, logits(q[h], k_far[h])))
+                groups.append((0, logits(q_b, k_far[h])))
             for j in range(n_q):
-                groups.append((j, logits(q[h][j * piece:], k_own[h][j * piece:(j + 1) * piece])))
+                groups.append((j, logits(q_b[j * piece:], k_b[j * piece:(j + 1) * piece])))
             scores.append(groups)
         v_own = dot(x_q, w_v[...]).astype(jnp.bfloat16)
         if mode == "far":
             v_far = dot(x_far, w_v[...]).astype(jnp.bfloat16)
-        for h in range(2):
+        tops = [None, None]
+        rows = lax.broadcasted_iota(jnp.int32, (CHUNK, piece), 0)
+        lanes = lax.broadcasted_iota(jnp.int32, (CHUNK, piece), 1)
+        for (b, h), groups in zip(units, scores):
             cols = slice(h * HEAD_DIM, (h + 1) * HEAD_DIM)
             values = [v_far[:, cols]] if mode == "far" else []
-            values += [v_own[j * piece:(j + 1) * piece, cols] for j in range(n_q)]
+            values += [v_own[b * span + j * piece:b * span + (j + 1) * piece, cols] for j in range(n_q)]
             probs = [[] for _ in values]
-            inverse, best = [], None
-            for i in range(n_q):
+            inverse = []
+            for at in range(0, span, CHUNK):
+                i = at // piece
                 parts = []
-                for g, (start, s) in enumerate(scores[h]):
+                for g, (start, s) in enumerate(groups):
                     if start <= i:
-                        part = s[(i - start) * piece:(i - start + 1) * piece]
-                        diagonal = g == len(scores[h]) - n_q + i
-                        parts.append((g, jnp.where(causal, part, NEG) if diagonal else part))
+                        part = s[at - start * piece:at - start * piece + CHUNK]
+                        diagonal = g == len(groups) - n_q + i
+                        parts.append((g, jnp.where(rows + (at - i * piece) >= lanes, part, NEG) if diagonal else part))
                 m = functools.reduce(jnp.maximum, [jnp.max(part, axis=1, keepdims=True) for _, part in parts])
                 total = None
                 for g, part in parts:
@@ -129,18 +144,18 @@
                     total = add if total is None else total + add
                     probs[g].append(p.astype(jnp.bfloat16))
                 inverse.append(1.0 / total)
-                m_top = jnp.max(m)
-                best = m_top if best is None else jnp.maximum(best, m_top)
+                tops[h] = m if tops[h] is None else jnp.maximum(tops[h], m)
             weighted = [dot(jnp.concatenate(p, axis=0), v) for p, v in zip(probs, values)]
             col = pl.ds(pl.multiple_of(step * GROUP + h * HEAD_DIM, HEAD_DIM), HEAD_DIM)
-            for i in range(n_q):
+            for n, at in enumerate(range(0, span, CHUNK)):
                 acc = None
-                for (start, _), w in zip(scores[h], weighted):
-                    if start <= i:
-                        part = w[(i - start) * piece:(i - start + 1) * piece]
+                for (start, _), w in zip(groups, weighted):
+                    if start * piece <= at:
+                        part = w[at - start * piece:at - start * piece + CHUNK]
                         acc = part if acc is None else acc + part
-                att[i * piece:(i + 1) * piece, col] = (acc * inverse[i]).astype(jnp.bfloat16)
-            top[0, 0, h, :] = jnp.full((top.shape[3],), best * scale, jnp.float32)
+                att[b * span + at:b * span + at + CHUNK, col] = (acc * inverse[n]).astype(jnp.bfloat16)
+        for h in range(2):
+            top[0, 0, h, :] = jnp.full((top.shape[3],), jnp.max(tops[h]) * scale, jnp.float32)
 
     top[...] = jnp.full(top.shape, -jnp.inf, jnp.float32)
 
@@ -184,24 +199,25 @@
     any_spec = pl.BlockSpec(memory_space=pl.ANY)
     w_spec = pl.BlockSpec((d_model, GROUP), lambda r, g, m: (0, jnp.where(m[0] == active, g, 0)))
     t_spec = pl.BlockSpec(tables[0].shape, lambda r, g, m: (0, 0), pipeline_mode=pl.Buffered(1))
-    n_q = 4 if mode == "whole" else 2
-    x_len = (2 if mode == "near" else 4) * piece
+    pack = PACK[mode]
+    n_q = pack * (4 if mode == "whole" else 2)
+    x_len = 4 * piece
     if mode == "whole":
         out_shape = [jax.ShapeDtypeStruct((n_rows, piece, d_model), jnp.bfloat16)] * 4
     else:
         out_shape = [jax.ShapeDtypeStruct(hidden.shape, jnp.bfloat16), jax.ShapeDtypeStruct(sib.shape, jnp.bfloat16)]
     n_dst = len(out_shape)
-    out_shape = out_shape + [jax.ShapeDtypeStruct((n_rows, n_steps, 8, 128), jnp.float32)]
+    out_shape = out_shape + [jax.ShapeDtypeStruct((n_rows // pack, n_steps, 8, 128), jnp.float32)]
     n_in = 2 + len(remote) + 6
     blocks = {"near": 3, "far": 7, "whole": 10}[mode]
     projections = {"near": 2 * 4, "far": 2 * 6, "whole": 4 * 4}[mode]
     flops = n_rows * (2 * projections * piece * d_model * width + 8 * blocks * piece * piece * width)
-    return pl.pallas_call(
+    *results, top = pl.pallas_call(
         functools.partial(rows_kernel, mode, first_row),
         out_shape=out_shape,
         grid_spec=pltpu.PrefetchScalarGridSpec(
             num_scalar_prefetch=1,
-            grid=(n_rows, n_steps),
+            grid=(n_rows // pack, n_steps),
             in_specs=[any_spec] * (2 + len(remote)) + [w_spec] * 3 + [any_spec, t_spec, t_spec] + [any_spec] * len(chain),
             out_specs=[any_spec] * n_dst + [pl.BlockSpec((1, 1, 8, 128), lambda r, g, m: (r, g, 0, 0))],
             scratch_shapes=[
@@ -216,6 +232,7 @@
         cost_estimate=pl.CostEstimate(flops=flops, bytes_accessed=40_000_000 * n_rows, transcendentals=0),
         input_output_aliases={1 + n_in + n: n for n in range(len(chain))},
     )(meta, hidden, sib, *remote, w_q, w_k, w_v, w_o, *tables, *chain)
+    return *results, top.max(axis=0, keepdims=True)
 
 
 def clip_weights(head_max, w_q, w_k):
@@ -247,13 +264,15 @@
             return lax.dynamic_slice_in_dim(array, which * half + row, 1, axis=0)
 
         mine, other = {}, {}
-        later = hidden
-        for rows in ([0], [kept], [r for r in range(half) if r not in (0, kept)]):
+        sib = lax.dynamic_slice_in_dim(hidden, (1 - core) * half, half, axis=0)
+        later, sib = lax.optimization_barrier((hidden, sib))
+        sib = send(sib, in_chip)
+        early = [0, 1, kept]
+        for rows in ([0], early[1:], [r for r in range(half) if r not in early]):
             fetched = [row_of(later, which, r) for r in rows for which in (core, 1 - core)]
             later, *fetched = lax.optimization_barrier((later, *fetched))
             for n, r in enumerate(rows):
                 mine[r], other[r] = fetched[2 * n], fetched[2 * n + 1]
-        sib = send(lax.dynamic_slice_in_dim(later, (1 - core) * half, half, axis=0), in_chip)
         remote = []
         for r in range(half):
             straight, cross = up if r < kept else down
@@ -281,8 +300,8 @@
             pass_on = jnp.where(chip == 1, send(cross, up[1]), pass_on)
             out = lax.dynamic_update_slice_in_dim(out, keep, core * half + r, axis=0)
             out = lax.dynamic_update_slice_in_dim(out, pass_on, (1 - core) * half + r, axis=0)
-        tops = jnp.concatenate([top.max(axis=0)[None, :, :2, 0] for top in tops], axis=0)
-        head_max = lax.pmax(lax.pmax(tops.max(axis=0).reshape(-1), "cp"), "dp")
+        head_max = functools.reduce(jnp.maximum, tops)[0, :, :2, 0].reshape(-1)
+        head_max = lax.pmax(lax.all_gather(head_max, "cp").max(axis=0), "dp")
         w_q_new, w_k_new = clip_weights(head_max, w_q, w_k)
         return out, head_max, w_q_new, w_k_new
 

time: 668 us -> 641 us (0.960)
  Pallas kernels: 402 us -> 384 us
    pallas_call x10, Pallas kernels: 402 us -> 384 us  [rows_call(): pl.pallas_call(functools.partial(rows_kernel, mode, first_row), out_shape...]
    pmax x2 -> x1, blocking collectives: 30.7 us -> 21.7 us  [layer(): head_max = lax.pmax(lax.all_gather(head_max, 'cp').max(axis=0), 'dp')]
  transfers between devices with their start and end apart: 24 -> 24, of which waited for: 7 -> 7; matrix products, arithmetic and copies ran while one was open for 4% -> 7% of each run, Pallas kernels for 61% -> 60%
where the time goes in v3:
time: 641 us; the launch traced here: 636 us
  Pallas kernels  384 us (60%)
  waiting for transfers between devices  117 us (18%)
  starting transfers between devices  44.6 us (7%)
  blocking collectives  33.7 us (5%)
  local copies, waits for them, and re-layouts  30.9 us (5%)
  other arithmetic  23.8 us (4%)
    pallas_call x10, Pallas kernels, rows_call(): pl.pallas_call(functools.partial(rows_kernel, mode, first_row), out_shape...  384 us
    ppermute x24, waiting for transfers between devices, send(): return lax.ppermute(x, 'cp', pairs)  117 us
    ppermute x24, starting transfers between devices, send(): return lax.ppermute(x, 'cp', pairs)  44.6 us
    pmax x1, blocking collectives, layer(): head_max = lax.pmax(lax.all_gather(head_max, 'cp').max(axis=0), 'dp')  21.7 us
    dynamic_slice x3, local copies, waits for them, and re-layouts, row_of(): return lax.dynamic_slice_in_dim(array, which * half + row, 1, axis=0)  15.6 us
    convert_element_type x1, other arithmetic, clip_weights(): (w_k.astype(jnp.float32) * col_factor).astype(jnp.bfloat16)  13.4 us
  transfers between devices with their start and end apart: 24, of which 7 were waited for; matrix products, arithmetic and copies ran while one was open for 7% of the time, Pallas kernels for 60%

profile of v3, /device:TPU:0, one launch (start us, length us, event | category | flops | bytes accessed | tf_op | source)
XLA Modules:
  0.0 635.5 jit_solution(6109673099963239903)
XLA Ops:
  0.6 6.3 all-gather
  6.9 8.4 %constant_dynamic-slice_fusion.16 = bf16[8,256,2048]{2,1,0:T(8,128)(2,1)} fusion(bf16[16,256,2048]{2,1,0:T(8,128)(2,1)} %hidden.9, s32[]{:T(128)S(6)} %select_n.91), kind=kLoop, calls=%fused_computation.36 | loop fusion | bytes 16777220 | tf_op jit(solution)/shard_map/dynamic_slice | solution.py:267
  15.7 3.1 constant_dynamic-slice_fusion.14
  18.9 4.8 collective-permute-start.11
  23.7 2.3 collective-permute-start.12
  26.0 4.4 constant_dynamic-slice_fusion.10
  30.4 2.3 collective-permute-start.10
  32.6 2.3 collective-permute-start.9
  34.9 8.1 %constant_dynamic-slice_fusion = (bf16[1,256,2048]{2,1,0:T(8,128)(2,1)}, bf16[1,256,2048]{2,1,0:T(8,128)(2,1)}, bf16[1,256,2048]{2,1,0:T(8,128)(2,1)}, bf16[1,25...) fusion(bf16[16,256,2048]{2,1,0:T(8,128)(2,1)} %hidden.9, ...), kind=kLoop, calls=%fused_computation.20 | loop fusion | bytes 20971560 | tf_op jit(solution)/shard_map/dynamic_slice | solution.py:264
  43.7 1.9 fusion
  45.6 1.3 pad_maximum_fusion
  46.9 2.4 collective-permute-start.7
  49.3 69.0 %shard_map.93 = (bf16[16,256,2048]{2,1,0:T(8,128)(2,1)}, bf16[8,256,2048]{2,1,0:T(8,128)(2,1)}, f32[1,8,8,128]{3,2,1,0:T(8,128)}) custom-call(s32[2]{0:T(128)} %pad_add_fusion.meta, bf16[16,256,2048]{2,1,0:T(8,128)(2,1)} %hidden.9, bf16[8,256,2048]{2,1,0:T(8,128)(2,1)} %collective-permute-done.sib, bf16[2048,2048]{1,0:T(8,128)(2,1)} %refs_2_.19, ...), custom_call_target="tpu_custom_call" | custom-call | flops 40802189312 | bytes 80000000 | tf_op jit(solution)/shard_map/pallas_call | solution.py:215
  118.3 2.3 collective-permute-start.8
  120.6 2.5 collective-permute-start.5
  123.1 5.4 shard_map.94
  128.6 2.3 collective-permute-start.6
  130.8 2.7 collective-permute-start.3
  133.6 5.4 shard_map.95
  139.0 132.6 %shard_map.96 = (bf16[16,256,2048]{2,1,0:T(8,128)(2,1)}, bf16[8,256,2048]{2,1,0:T(8,128)(2,1)}, f32[2,8,8,128]{3,2,1,0:T(8,128)}) custom-call(s32[2]{0:T(128)} %pad_add_fusion.meta, bf16[16,256,2048]{2,1,0:T(8,128)(2,1)} %hidden.9, bf16[8,256,2048]{2,1,0:T(8,128)(2,1)} %collective-permute-done.sib, ...), custom_call_target="tpu_custom_call", output_to_operand_aliasing={{0}: (9, {}), {1}: (10, {})} | custom-call | flops 81604378624 | bytes 160000000 | tf_op jit(solution)/shard_map/pallas_call | solution.py:215
  271.6 2.3 collective-permute-start.4
  273.9 2.3 collective-permute-start.1
  276.1 5.6 shard_map.97
  281.8 2.3 collective-permute-start.2
  285.4 5.7 shard_map.98
  292.3 4.4 collective-permute-done.4.refs_1_
  298.0 5.9 shard_map.99
  303.9 15.3 %collective-permute-done.1.refs_0_ = bf16[1,256,2048]{2,1,0:T(8,128)(2,1)} collective-permute-done((bf16[1,256,2048]{2,1,0:T(8,128)(2,1)}, bf16[1,256,2048]{2,1,0:T(8,128)(2,1)}, u32[]{:S(2)}, u32[]{:S(2)}) %collective-permute-start.1) | collective-permute-done | bytes 1048608 | tf_op jit(solution)/shard_map/ppermute | solution.py:258
  320.5 20.4 %collective-permute-done.2.refs_1_ = bf16[1,256,2048]{2,1,0:T(8,128)(2,1)} collective-permute-done((bf16[1,256,2048]{2,1,0:T(8,128)(2,1)}, bf16[1,256,2048]{2,1,0:T(8,128)(2,1)}, u32[]{:S(2)}, u32[]{:S(2)}) %collective-permute-start.2) | collective-permute-done | bytes 1048608 | tf_op jit(solution)/shard_map/ppermute | solution.py:258
  340.9 5.6 shard_map.100
  346.6 19.8 %collective-permute-done.20.refs_1_ = bf16[1,256,2048]{2,1,0:T(8,128)(2,1)} collective-permute-done((bf16[1,256,2048]{2,1,0:T(8,128)(2,1)}, bf16[1,256,2048]{2,1,0:T(8,128)(2,1)}, u32[]{:S(2)}, u32[]{:S(2)}) %collective-permute-start.20) | collective-permute-done | bytes 1048608 | tf_op jit(solution)/shard_map/ppermute | solution.py:258
  366.4 74.4 %shard_map.102 = (bf16[1,256,2048]{2,1,0:T(8,128)(2,1)}, bf16[1,256,2048]{2,1,0:T(8,128)(2,1)}, bf16[1,256,2048]{2,1,0:T(8,128)(2,1)}, bf16[1,256,2048]{2,1,0:T(8,128)(2,1)}, f32[1,8,8,128]{3,2,1,0:T(8,128)}) custom-call(s32[2]{0:T(128)} %pad_add_fusion.meta, bf16[16,256,2048]{2,1,0:T(8,128)(2,1)} %hidden.9, bf16[8,256,2048]{2,1,0:T(8,128)(2,1)} %collective-permute-done.sib, ...), custom_call_target="tpu_custom_call" | custom-call | flops 45097156608 | bytes 40000000 | tf_op jit(solution)/shard_map/pallas_call | solution.py:215
  440.8 74.4 %shard_map.101 = (bf16[1,256,2048]{2,1,0:T(8,128)(2,1)}, bf16[1,256,2048]{2,1,0:T(8,128)(2,1)}, bf16[1,256,2048]{2,1,0:T(8,128)(2,1)}, bf16[1,256,2048]{2,1,0:T(8,128)(2,1)}, f32[1,8,8,128]{3,2,1,0:T(8,128)}) custom-call(s32[2]{0:T(128)} %pad_add_fusion.meta, bf16[16,256,2048]{2,1,0:T(8,128)(2,1)} %hidden.9, bf16[8,256,2048]{2,1,0:T(8,128)(2,1)} %collective-permute-done.sib, ...), custom_call_target="tpu_custom_call" | custom-call | flops 45097156608 | bytes 40000000 | tf_op jit(solution)/shard_map/pallas_call | solution.py:215
  516.3 5.7 all-gather.1
  522.0 21.7 %pmax.7 = f32[16]{0:T(128)S(1)} all-reduce(f32[16]{0:T(128)S(1)} %reduce_max.23), channel_id=1, replica_groups=mesh['dp'=8,'cp'=4] {'dp'}, use_global_device_ids=true, to_apply=%region_2.3 | all-reduce | flops 16 | bytes 128 | tf_op jit(solution)/shard_map/pmax | solution.py:304
  543.7 3.3 collective-permute-start.16
  547.1 13.4 %multiply_convert_fusion = (bf16[2048,2048]{1,0:T(8,128)(2,1)}, bf16[2048,2048]{1,0:T(8,128)(2,1)}) fusion(bf16[2048,2048]{1,0:T(8,128)(2,1)} %refs_3_.19, f32[2048]{0:T(1024)S(1)} %broadcast_bitcast_fusion, bf16[2048,2048]{1,0:T(8,128)(2,1)} %refs_2_.19), kind=kLoop, calls=%fused_computation | loop fusion | flops 25165824 | bytes 33562624 | tf_op jit(solution)/shard_map/convert_element_type | solution.py:241
  560.6 1.8 collective-permute-start.17
  562.5 1.3 collective-permute-start.21
  563.9 1.4 collective-permute-start.22
  565.2 6.6 %slice_dynamic-update-slice_fusion = bf16[16,256,2048]{2,1,0:T(8,128)(2,1)} fusion(bf16[16,256,2048]{2,1,0:T(8,128)(2,1)} %get-tuple-element.92, s32[]{:T(128)S(6)} %select_n.91, bf16[8,256,2048]{2,1,0:T(8,128)(2,1)} %collective-permute-done.13), kind=kLoop, calls=%fused_computation.2 | loop fusion | bytes 12582916 | tf_op jit(solution)/shard_map/dynamic_update_slice | solution.py:295
  572.3 1.4 select_dynamic-update-slice_fusion.3
  573.7 18.9 %collective-permute-done.17 = bf16[1,256,2048]{2,1,0:T(8,128)(2,1)S(1)} collective-permute-done((bf16[1,256,2048]{2,1,0:T(8,128)(2,1)S(1)}, bf16[1,256,2048]{2,1,0:T(8,128)(2,1)S(1)}, u32[]{:S(2)}, u32[]{:S(2)}) %collective-permute-start.17) | collective-permute-done | bytes 1048608 | tf_op jit(solution)/shard_map/ppermute | solution.py:258
  592.6 1.4 select_dynamic-update-slice_fusion.2
  594.0 21.1 %collective-permute-done.21 = bf16[1,256,2048]{2,1,0:T(8,128)(2,1)S(1)} collective-permute-done((bf16[1,256,2048]{2,1,0:T(8,128)(2,1)S(1)}, bf16[1,256,2048]{2,1,0:T(8,128)(2,1)S(1)}, u32[]{:S(2)}, u32[]{:S(2)}) %collective-permute-start.21) | collective-permute-done | bytes 1048608 | tf_op jit(solution)/shard_map/ppermute | solution.py:258
  615.1 1.4 select_dynamic-update-slice_fusion.1
  616.4 17.2 %collective-permute-done.22 = bf16[1,256,2048]{2,1,0:T(8,128)(2,1)S(1)} collective-permute-done((bf16[1,256,2048]{2,1,0:T(8,128)(2,1)S(1)}, bf16[1,256,2048]{2,1,0:T(8,128)(2,1)S(1)}, u32[]{:S(2)}, u32[]{:S(2)}) %collective-permute-start.22) | collective-permute-done | bytes 1048608 | tf_op jit(solution)/shard_map/ppermute | solution.py:258
  633.7 1.4 select_dynamic-update-slice_fusion
  (59 shorter events, 8.0 us)
Async XLA Ops:
  15.4 31.5 %collective-permute-start = (bf16[8,256,2048]{2,1,0:T(8,128)(2,1)}, bf16[8,256,2048]{2,1,0:T(8,128)(2,1)}, u32[]{:S(2)}, u32[]{:S(2)}) collective-permute-start(bf16[8,256,2048]{2,1,0:T(8,128)(2,1)} %constant_dynamic-slice_fusion.16), channel_id=1, source_target_pairs={{0,1},{1,0},{2,3},{3,2},{4,5},{5,4},{6,7},{7,6},{8,9},{9,8},{10,11... | collective-permute-start | bytes 25165832 | tf_op jit(solution)/shard_map/ppermute | solution.py:258
  18.9 99.4 %collective-permute-start.11 = (bf16[1,256,2048]{2,1,0:T(8,128)(2,1)}, bf16[1,256,2048]{2,1,0:T(8,128)(2,1)}, u32[]{:S(2)}, u32[]{:S(2)}) collective-permute-start(bf16[1,256,2048]{2,1,0:T(8,128)(2,1)} %get-tuple-element.76), channel_id=1, source_target_pairs={{0,2},{1,3},{4,6},{5,7},{8,10},{9,11},{12,14},{13,15},{16,18},{17,... | collective-permute-start | bytes 3145736 | tf_op jit(solution)/shard_map/ppermute | solution.py:258
  23.7 96.9 %collective-permute-start.12 = (bf16[1,256,2048]{2,1,0:T(8,128)(2,1)}, bf16[1,256,2048]{2,1,0:T(8,128)(2,1)}, u32[]{:S(2)}, u32[]{:S(2)}) collective-permute-start(bf16[1,256,2048]{2,1,0:T(8,128)(2,1)} %get-tuple-element.77), channel_id=1, source_target_pairs={{0,3},{1,2},{4,7},{5,6},{8,11},{9,10},{12,15},{13,14},{16,19},{17,... | collective-permute-start | bytes 3145736 | tf_op jit(solution)/shard_map/ppermute | solution.py:258
  30.4 98.2 %collective-permute-start.10 = (bf16[1,256,2048]{2,1,0:T(8,128)(2,1)}, bf16[1,256,2048]{2,1,0:T(8,128)(2,1)}, u32[]{:S(2)}, u32[]{:S(2)}) collective-permute-start(bf16[1,256,2048]{2,1,0:T(8,128)(2,1)} %get-tuple-element.75), channel_id=1, source_target_pairs={{0,3},{1,2},{4,7},{5,6},{8,11},{9,10},{12,15},{13,14},{16,19},{17,... | collective-permute-start | bytes 3145736 | tf_op jit(solution)/shard_map/ppermute | solution.py:258
  32.6 98.2 %collective-permute-start.9 = (bf16[1,256,2048]{2,1,0:T(8,128)(2,1)}, bf16[1,256,2048]{2,1,0:T(8,128)(2,1)}, u32[]{:S(2)}, u32[]{:S(2)}) collective-permute-start(bf16[1,256,2048]{2,1,0:T(8,128)(2,1)} %get-tuple-element.74), channel_id=1, source_target_pairs={{0,2},{1,3},{4,6},{5,7},{8,10},{9,11},{12,14},{13,15},{16,18},{17,... | collective-permute-start | bytes 3145736 | tf_op jit(solution)/shard_map/ppermute | solution.py:258
  46.9 224.7 %collective-permute-start.7 = (bf16[1,256,2048]{2,1,0:T(8,128)(2,1)}, bf16[1,256,2048]{2,1,0:T(8,128)(2,1)}, u32[]{:S(2)}, u32[]{:S(2)}) collective-permute-start(bf16[1,256,2048]{2,1,0:T(8,128)(2,1)} %get-tuple-element.72), channel_id=1, source_target_pairs={{0,2},{1,3},{4,6},{5,7},{8,10},{9,11},{12,14},{13,15},{16,18},{17,... | collective-permute-start | bytes 3145736 | tf_op jit(solution)/shard_map/ppermute | solution.py:258
  118.3 155.6 %collective-permute-start.8 = (bf16[1,256,2048]{2,1,0:T(8,128)(2,1)}, bf16[1,256,2048]{2,1,0:T(8,128)(2,1)}, u32[]{:S(2)}, u32[]{:S(2)}) collective-permute-start(bf16[1,256,2048]{2,1,0:T(8,128)(2,1)} %get-tuple-element.73), channel_id=1, source_target_pairs={{0,3},{1,2},{4,7},{5,6},{8,11},{9,10},{12,15},{13,14},{16,19},{17,... | collective-permute-start | bytes 3145736 | tf_op jit(solution)/shard_map/ppermute | solution.py:258
  120.6 161.1 %collective-permute-start.5 = (bf16[1,256,2048]{2,1,0:T(8,128)(2,1)}, bf16[1,256,2048]{2,1,0:T(8,128)(2,1)}, u32[]{:S(2)}, u32[]{:S(2)}) collective-permute-start(bf16[1,256,2048]{2,1,0:T(8,128)(2,1)} %get-tuple-element.70), channel_id=1, source_target_pairs={{0,2},{1,3},{4,6},{5,7},{8,10},{9,11},{12,14},{13,15},{16,18},{17,... | collective-permute-start | bytes 3145736 | tf_op jit(solution)/shard_map/ppermute | solution.py:258
  128.6 155.5 %collective-permute-start.6 = (bf16[1,256,2048]{2,1,0:T(8,128)(2,1)}, bf16[1,256,2048]{2,1,0:T(8,128)(2,1)}, u32[]{:S(2)}, u32[]{:S(2)}) collective-permute-start(bf16[1,256,2048]{2,1,0:T(8,128)(2,1)} %get-tuple-element.71), channel_id=1, source_target_pairs={{0,3},{1,2},{4,7},{5,6},{8,11},{9,10},{12,15},{13,14},{16,19},{17,... | collective-permute-start | bytes 3145736 | tf_op jit(solution)/shard_map/ppermute | solution.py:258
  130.8 160.2 %collective-permute-start.3 = (bf16[1,256,2048]{2,1,0:T(8,128)(2,1)}, bf16[1,256,2048]{2,1,0:T(8,128)(2,1)}, u32[]{:S(2)}, u32[]{:S(2)}) collective-permute-start(bf16[1,256,2048]{2,1,0:T(8,128)(2,1)} %get-tuple-element.68), channel_id=1, source_target_pairs={{0,2},{1,3},{4,6},{5,7},{8,10},{9,11},{12,14},{13,15},{16,18},{17,... | collective-permute-start | bytes 3145736 | tf_op jit(solution)/shard_map/ppermute | solution.py:258
  271.6 25.1 %collective-permute-start.4 = (bf16[1,256,2048]{2,1,0:T(8,128)(2,1)}, bf16[1,256,2048]{2,1,0:T(8,128)(2,1)}, u32[]{:S(2)}, u32[]{:S(2)}) collective-permute-start(bf16[1,256,2048]{2,1,0:T(8,128)(2,1)} %get-tuple-element.69), channel_id=1, source_target_pairs={{0,3},{1,2},{4,7},{5,6},{8,11},{9,10},{12,15},{13,14},{16,19},{17,... | collective-permute-start | bytes 3145736 | tf_op jit(solution)/shard_map/ppermute | solution.py:258
  273.9 45.3 %collective-permute-start.1 = (bf16[1,256,2048]{2,1,0:T(8,128)(2,1)}, bf16[1,256,2048]{2,1,0:T(8,128)(2,1)}, u32[]{:S(2)}, u32[]{:S(2)}) collective-permute-start(bf16[1,256,2048]{2,1,0:T(8,128)(2,1)} %get-tuple-element.65), channel_id=1, source_target_pairs={{0,2},{1,3},{4,6},{5,7},{8,10},{9,11},{12,14},{13,15},{16,18},{17,... | collective-permute-start | bytes 3145736 | tf_op jit(solution)/shard_map/ppermute | solution.py:258
  281.8 59.1 %collective-permute-start.2 = (bf16[1,256,2048]{2,1,0:T(8,128)(2,1)}, bf16[1,256,2048]{2,1,0:T(8,128)(2,1)}, u32[]{:S(2)}, u32[]{:S(2)}) collective-permute-start(bf16[1,256,2048]{2,1,0:T(8,128)(2,1)} %get-tuple-element.66), channel_id=1, source_target_pairs={{0,3},{1,2},{4,7},{5,6},{8,11},{9,10},{12,15},{13,14},{16,19},{17,... | collective-permute-start | bytes 3145736 | tf_op jit(solution)/shard_map/ppermute | solution.py:258
  284.1 62.5 %collective-permute-start.19 = (bf16[1,256,2048]{2,1,0:T(8,128)(2,1)}, bf16[1,256,2048]{2,1,0:T(8,128)(2,1)}, u32[]{:S(2)}, u32[]{:S(2)}) collective-permute-start(bf16[1,256,2048]{2,1,0:T(8,128)(2,1)} %get-tuple-element.100), channel_id=1, source_target_pairs={{2,0},{3,1},{6,4},{7,5},{10,8},{11,9},{14,12},{15,13},{18,16},{19,... | collective-permute-start | bytes 3145736 | tf_op jit(solution)/shard_map/ppermute | solution.py:258
  291.0 75.4 %collective-permute-start.20 = (bf16[1,256,2048]{2,1,0:T(8,128)(2,1)}, bf16[1,256,2048]{2,1,0:T(8,128)(2,1)}, u32[]{:S(2)}, u32[]{:S(2)}) collective-permute-start(bf16[1,256,2048]{2,1,0:T(8,128)(2,1)} %get-tuple-element.101), channel_id=1, source_target_pairs={{2,1},{3,0},{6,5},{7,4},{10,9},{11,8},{14,13},{15,12},{18,17},{19,... | collective-permute-start | bytes 3145736 | tf_op jit(solution)/shard_map/ppermute | solution.py:258
  296.8 144.1 %collective-permute-start.14 = (bf16[1,256,2048]{2,1,0:T(8,128)(2,1)}, bf16[1,256,2048]{2,1,0:T(8,128)(2,1)}, u32[]{:S(2)}, u32[]{:S(2)}) collective-permute-start(bf16[1,256,2048]{2,1,0:T(8,128)(2,1)} %get-tuple-element.94), channel_id=1, source_target_pairs={{2,0},{3,1},{6,4},{7,5},{10,8},{11,9},{14,12},{15,13},{18,16},{19,... | collective-permute-start | bytes 3145736 | tf_op jit(solution)/shard_map/ppermute | solution.py:258
  319.2 121.6 %collective-permute-start.15 = (bf16[1,256,2048]{2,1,0:T(8,128)(2,1)}, bf16[1,256,2048]{2,1,0:T(8,128)(2,1)}, u32[]{:S(2)}, u32[]{:S(2)}) collective-permute-start(bf16[1,256,2048]{2,1,0:T(8,128)(2,1)} %get-tuple-element.95), channel_id=1, source_target_pairs={{2,1},{3,0},{6,5},{7,4},{10,9},{11,8},{14,13},{15,12},{18,17},{19,... | collective-permute-start | bytes 3145736 | tf_op jit(solution)/shard_map/ppermute | solution.py:258
  346.5 94.3 %copy-start.2 = (f32[2,8,8,128]{3,2,1,0:T(8,128)S(1)}, f32[2,8,8,128]{3,2,1,0:T(8,128)}, u32[]{:S(2)}) copy-start(f32[2,8,8,128]{3,2,1,0:T(8,128)} %get-tuple-element.109) | copy-start | bytes 196612
  346.5 94.3 %copy-start.3 = (f32[1,8,8,128]{3,2,1,0:T(8,128)S(1)}, f32[1,8,8,128]{3,2,1,0:T(8,128)}, u32[]{:S(2)}) copy-start(f32[1,8,8,128]{3,2,1,0:T(8,128)} %get-tuple-element.106) | copy-start | bytes 98308
  346.5 94.3 %copy-start.4 = (f32[1,8,8,128]{3,2,1,0:T(8,128)S(1)}, f32[1,8,8,128]{3,2,1,0:T(8,128)}, u32[]{:S(2)}) copy-start(f32[1,8,8,128]{3,2,1,0:T(8,128)} %get-tuple-element.107) | copy-start | bytes 98308
  346.5 94.3 %copy-start.5 = (f32[1,8,8,128]{3,2,1,0:T(8,128)S(1)}, f32[1,8,8,128]{3,2,1,0:T(8,128)}, u32[]{:S(2)}) copy-start(f32[1,8,8,128]{3,2,1,0:T(8,128)} %get-tuple-element.108) | copy-start | bytes 98308
  346.5 217.3 %collective-permute-start.13 = (bf16[8,256,2048]{2,1,0:T(8,128)(2,1)}, bf16[8,256,2048]{2,1,0:T(8,128)(2,1)}, u32[]{:S(2)}, u32[]{:S(2)}) collective-permute-start(bf16[8,256,2048]{2,1,0:T(8,128)(2,1)} %get-tuple-element.93), channel_id=1, source_target_pairs={{0,1},{1,0},{2,3},{3,2},{4,5},{5,4},{6,7},{7,6},{8,9},{9,8},{10,11... | collective-permute-start | bytes 25165832 | tf_op jit(solution)/shard_map/ppermute | solution.py:258
  543.7 16.8 %copy-start.11 = (f32[16]{0:T(128)}, f32[16]{0:T(128)S(1)}, u32[]{:S(2)}) copy-start(f32[16]{0:T(128)S(1)} %pmax.7) | copy-start | bytes 196
  543.7 28.1 %collective-permute-start.16 = (bf16[1,256,2048]{2,1,0:T(8,128)(2,1)}, bf16[1,256,2048]{2,1,0:T(8,128)(2,1)S(1)}, u32[]{:S(2)}, u32[]{:S(2)}) collective-permute-start(bf16[1,256,2048]{2,1,0:T(8,128)(2,1)} %get-tuple-element.96), channel_id=1, source_target_pairs={{0,2},{1,3},{4,6},{5,7},{8,10},{9,11},{12,14},{13,15},{16,18},{17,... | collective-permute-start | bytes 3145736 | tf_op jit(solution)/shard_map/ppermute | solution.py:258
  547.1 13.5 %copy-start.10 = (bf16[1,256,2048]{2,1,0:T(8,128)(2,1)S(1)}, bf16[1,256,2048]{2,1,0:T(8,128)(2,1)}, u32[]{:S(2)}) copy-start(bf16[1,256,2048]{2,1,0:T(8,128)(2,1)} %get-tuple-element.98) | copy-start | bytes 3145732
  547.1 15.3 %copy-start.9 = (bf16[1,256,2048]{2,1,0:T(8,128)(2,1)S(1)}, bf16[1,256,2048]{2,1,0:T(8,128)(2,1)}, u32[]{:S(2)}) copy-start(bf16[1,256,2048]{2,1,0:T(8,128)(2,1)} %get-tuple-element.99) | copy-start | bytes 3145732
  547.1 15.4 %copy-start.8 = (bf16[1,256,2048]{2,1,0:T(8,128)(2,1)S(1)}, bf16[1,256,2048]{2,1,0:T(8,128)(2,1)}, u32[]{:S(2)}) copy-start(bf16[1,256,2048]{2,1,0:T(8,128)(2,1)} %get-tuple-element.102) | copy-start | bytes 3145732
  547.1 16.8 %copy-start.7 = (bf16[1,256,2048]{2,1,0:T(8,128)(2,1)S(1)}, bf16[1,256,2048]{2,1,0:T(8,128)(2,1)}, u32[]{:S(2)}) copy-start(bf16[1,256,2048]{2,1,0:T(8,128)(2,1)} %get-tuple-element.104) | copy-start | bytes 3145732
  547.1 24.8 %copy-start.6 = (bf16[1,256,2048]{2,1,0:T(8,128)(2,1)S(1)}, bf16[1,256,2048]{2,1,0:T(8,128)(2,1)}, u32[]{:S(2)}) copy-start(bf16[1,256,2048]{2,1,0:T(8,128)(2,1)} %get-tuple-element.105) | copy-start | bytes 3145732
  547.1 25.2 %copy-start.1 = (bf16[1,256,2048]{2,1,0:T(8,128)(2,1)S(1)}, bf16[1,256,2048]{2,1,0:T(8,128)(2,1)}, u32[]{:S(2)}) copy-start(bf16[1,256,2048]{2,1,0:T(8,128)(2,1)} %get-tuple-element.97) | copy-start | bytes 3145732
  560.5 54.5 %copy-start = (bf16[1,256,2048]{2,1,0:T(8,128)(2,1)S(1)}, bf16[1,256,2048]{2,1,0:T(8,128)(2,1)}, u32[]{:S(2)}) copy-start(bf16[1,256,2048]{2,1,0:T(8,128)(2,1)} %get-tuple-element.103) | copy-start | bytes 3145732
  560.6 32.0 %collective-permute-start.17 = (bf16[1,256,2048]{2,1,0:T(8,128)(2,1)S(1)}, bf16[1,256,2048]{2,1,0:T(8,128)(2,1)S(1)}, u32[]{:S(2)}, u32[]{:S(2)}) collective-permute-start(bf16[1,256,2048]{2,1,0:T(8,128)(2,1)S(1)} %copy-done.10), channel_id=1, source_target_pairs={{0,3},{1,2},{4,7},{5,6},{8,11},{9,10},{12,15},{13,14},{16,19},{17,... | collective-permute-start | bytes 3145736 | tf_op jit(solution)/shard_map/ppermute | solution.py:258
  562.4 30.2 %collective-permute-start.18 = (bf16[1,256,2048]{2,1,0:T(8,128)(2,1)S(1)}, bf16[1,256,2048]{2,1,0:T(8,128)(2,1)S(1)}, u32[]{:S(2)}, u32[]{:S(2)}) collective-permute-start(bf16[1,256,2048]{2,1,0:T(8,128)(2,1)S(1)} %copy-done.9), channel_id=1, source_target_pairs={{0,1},{1,0},{2,3},{3,2},{4,5},{5,4},{6,7},{7,6},{8,9},{9,8},{10,11... | collective-permute-start | bytes 3145736 | tf_op jit(solution)/shard_map/ppermute | solution.py:258
  562.5 52.6 %collective-permute-start.21 = (bf16[1,256,2048]{2,1,0:T(8,128)(2,1)S(1)}, bf16[1,256,2048]{2,1,0:T(8,128)(2,1)S(1)}, u32[]{:S(2)}, u32[]{:S(2)}) collective-permute-start(bf16[1,256,2048]{2,1,0:T(8,128)(2,1)S(1)} %copy-done.8), channel_id=1, source_target_pairs={{0,2},{1,3},{4,6},{5,7},{8,10},{9,11},{12,14},{13,15},{16,18},{17,... | collective-permute-start | bytes 3145736 | tf_op jit(solution)/shard_map/ppermute | solution.py:258
  563.9 69.8 %collective-permute-start.22 = (bf16[1,256,2048]{2,1,0:T(8,128)(2,1)S(1)}, bf16[1,256,2048]{2,1,0:T(8,128)(2,1)S(1)}, u32[]{:S(2)}, u32[]{:S(2)}) collective-permute-start(bf16[1,256,2048]{2,1,0:T(8,128)(2,1)S(1)} %copy-done.7), channel_id=1, source_target_pairs={{0,3},{1,2},{4,7},{5,6},{8,11},{9,10},{12,15},{13,14},{16,19},{17,... | collective-permute-start | bytes 3145736 | tf_op jit(solution)/shard_map/ppermute | solution.py:258
  571.8 61.8 %collective-permute-start.23 = (bf16[1,256,2048]{2,1,0:T(8,128)(2,1)S(1)}, bf16[1,256,2048]{2,1,0:T(8,128)(2,1)S(1)}, u32[]{:S(2)}, u32[]{:S(2)}) collective-permute-start(bf16[1,256,2048]{2,1,0:T(8,128)(2,1)S(1)} %copy-done.6), channel_id=1, source_target_pairs={{0,1},{1,0},{2,3},{3,2},{4,5},{5,4},{6,7},{7,6},{8,9},{9,8},{10,11... | collective-permute-start | bytes 3145736 | tf_op jit(solution)/shard_map/ppermute | solution.py:258
